TPU v7x, 16 devices: a whole 2x2x2 slice. The times are simulated.
16 devices in a mesh: col: 2 (over z), row: 8 (over y, x, core).
Axes of the slice: x: 2, y: 2, z: 2, core: 2. Of those that a mesh axis runs over, the one named last changes fastest.
Arguments:
- mask: int32 [8192, 32768], P('row', 'col')
- user_emb: bfloat16 [8192, 128], P(('row', 'col'))
- item_emb: bfloat16 [32768, 128], P(('col', 'row'))
- queries: int32 [1024], replicated
Outputs:
- output 1: bfloat16 [8192, 128], P(('row', 'col'))
- output 2: bfloat16 [32768, 128], P(('col', 'row'))
- output 3: float32 [1024, 32768], P(None, ('col', 'row'))
All inputs are finite; a program needn't handle non-finite values.
Results may differ from a plain program's by a relative error of at most 0.00652722.
Values are sent between devices in bfloat16 or wider.
A program may use at most 1 GiB of HBM per device.

v0:
```python
import jax
import jax.numpy as jnp
from jax import lax
from jax.sharding import PartitionSpec as P

LAYERS = 3


def norm_block(mask_blk):
    deg_user = lax.psum(jnp.sum(mask_blk, axis=1), 'col')
    deg_item = lax.psum(jnp.sum(mask_blk, axis=0), 'row')
    inv_user = lax.rsqrt(jnp.maximum(deg_user, 1).astype(jnp.float32))
    inv_item = lax.rsqrt(jnp.maximum(deg_item, 1).astype(jnp.float32))
    return (inv_user[:, None] * mask_blk.astype(jnp.float32) * inv_item[None, :]).astype(jnp.bfloat16)


def query_scores(final_user, final_item, queries, shard_pos):
    rows_local = final_user.shape[0]
    local_idx = queries - shard_pos * rows_local
    owned = (local_idx >= 0) & (local_idx < rows_local)
    picked = jnp.take(final_user, jnp.clip(local_idx, 0, rows_local - 1), axis=0)
    picked = jnp.where(owned[:, None], picked, jnp.zeros_like(picked))
    picked = lax.psum(picked, ('row', 'col'))
    return lax.dot_general(picked, final_item, (((1,), (1,)), ((), ())), preferred_element_type=jnp.float32)


def solution(mesh):
    n_col = mesh.shape['col']
    contract_rows = (((0,), (0,)), ((), ()))

    def device_step(mask_blk, user_shard, item_shard, queries):
        norm_adj = norm_block(mask_blk)
        user_cur = user_shard
        item_cur = item_shard
        user_sum = user_shard.astype(jnp.float32)
        item_sum = item_shard.astype(jnp.float32)
        for layer_idx in range(LAYERS):
            item_panel = lax.all_gather(item_cur, 'row', axis=0, tiled=True)
            user_part = jnp.dot(norm_adj, item_panel, preferred_element_type=jnp.float32)
            user_next = lax.psum_scatter(user_part, 'col', scatter_dimension=0, tiled=True).astype(jnp.bfloat16)
            user_panel = lax.all_gather(user_cur, 'col', axis=0, tiled=True)
            item_part = lax.dot_general(norm_adj, user_panel, contract_rows, preferred_element_type=jnp.float32)
            item_next = lax.psum_scatter(item_part, 'row', scatter_dimension=0, tiled=True).astype(jnp.bfloat16)
            user_sum = user_sum + user_next.astype(jnp.float32)
            item_sum = item_sum + item_next.astype(jnp.float32)
            user_cur = user_next
            item_cur = item_next
        final_user = (user_sum / (LAYERS + 1)).astype(jnp.bfloat16)
        final_item = (item_sum / (LAYERS + 1)).astype(jnp.bfloat16)
        shard_pos = lax.axis_index('row') * n_col + lax.axis_index('col')
        scores = query_scores(final_user, final_item, queries, shard_pos)
        return final_user, final_item, scores

    return jax.shard_map(device_step, mesh=mesh, in_specs=(P('row', 'col'), P(('row', 'col'), None), P(('col', 'row'), None), P()), out_specs=(P(('row', 'col'), None), P(('col', 'row'), None), P(None, ('col', 'row'))), check_vma=False)
```

profile of v0, /device:TPU:0, one launch (start us, length us, event | category | flops | bytes accessed | tf_op | source)
XLA Modules:
  0.0 558.6 jit_solution(13599004821916059559)
XLA Ops:
  7.2 0.0 copy-start.6
  7.2 0.0 all-reduce.3.cloned.1.call-start
  7.2 21.5 %fusion.1 = (s32[1024]{0:T(1024)S(1)}, s32[16384]{0:T(1024)}) fusion(s32[1024,16384]{1,0:T(8,128)} %param.4), kind=kLoop, calls=%fused_computation.11 | loop fusion | flops 33537024 | bytes 67178496 | tf_op jit(solution)/shard_map/reduce_sum | solution.py:10
  28.7 0.0 all-reduce.3.cloned.1.call-update
  28.7 0.0 all-gather.4.cloned.1.call-start
  28.8 0.7 all-gather.4.cloned.1.call-update
  29.5 0.0 reduce-scatter.9.cloned.1.call-start
  29.5 5.6 %psum.21 = s32[1024]{0:T(1024)S(1)} all-reduce(s32[1024]{0:T(1024)S(1)} %get-tuple-element.3), channel_id=1, replica_groups=mesh['col'=2,'row'=8] {'col'}, use_global_device_ids=true, to_apply=%region_1.0 | all-reduce | flops 1024 | bytes 8192 | tf_op jit(solution)/shard_map/psum | solution.py:10
  35.1 0.0 copy-done.6
  35.1 5.6 %all_gather.19 = bf16[1024,128]{1,0:T(8,128)(2,1)S(1)} all-gather(bf16[512,128]{1,0:T(8,128)(2,1)S(1)} %copy-done.6), channel_id=1, replica_groups=mesh['col'=2,'row'=8] {'col'}, dimensions={0}, use_global_device_ids=true | all-gather | bytes 393216 | tf_op jit(solution)/shard_map/all_gather | solution.py:41
  40.7 36.5 %all-reduce.3.cloned.1.call-done = s32[16384]{0:T(1024)} async-done(((s32[16384]{0:T(1024)}), s32[16384]{0:T(1024)}) %all-reduce.3.cloned.1.call-update) | async-done | bytes 65552 | tf_op jit(solution)/shard_map/psum | solution.py:11
  77.2 0.9 convert_rsqrt_fusion
  78.1 32.9 %multiply_convert_fusion = bf16[1024,16384]{1,0:T(8,128)(2,1)} fusion(s32[1024,16384]{1,0:T(8,128)} %param.4, f32[16384]{0:T(1024)S(1)} %convert_rsqrt_fusion, f32[1024]{0:T(1024)S(1)} %convert_rsqrt_fusion.1), kind=kLoop, calls=%fused_computation.1 | loop fusion | flops 67108864 | bytes 100732928 | tf_op jit(solution)/shard_map/convert_element_type | solution.py:14
  111.0 17.1 %fusion.3 = f32[16384,128]{1,0:T(8,128)} fusion(bf16[1024,16384]{1,0:T(8,128)(2,1)} %multiply_convert_fusion, bf16[1024,128]{1,0:T(8,128)(2,1)S(1)} %all_gather.19), kind=kOutput, calls=%fused_computation.13 | convolution fusion | flops 4294967296 | bytes 42205184 | tf_op jit(solution)/shard_map/dot_general | solution.py:42
  128.2 0.0 reduce-scatter.9.cloned.1.call-update
  128.2 0.0 reduce-scatter.7.cloned.1.call-start
  128.2 0.0 all-gather.4.cloned.1.call-done
  128.3 16.9 %fusion.2 = f32[1024,128]{1,0:T(8,128)} fusion(bf16[1024,16384]{1,0:T(8,128)(2,1)} %multiply_convert_fusion, bf16[16384,128]{1,0:T(8,128)(2,1)} %all-gather.4.cloned.1.call-done), kind=kOutput, calls=%fused_computation.12 | convolution fusion | flops 4294967296 | bytes 38273024 | tf_op jit(solution)/shard_map/dot_general | solution.py:39
  145.2 0.0 reduce-scatter.7.cloned.1.call-update
  145.2 0.0 all-gather.6.cloned.1.call-start
  145.2 47.5 %reduce-scatter.9.cloned.1.call-done = f32[2048,128]{1,0:T(8,128)} async-done(((f32[16384,128]{1,0:T(8,128)}), f32[2048,128]{1,0:T(8,128)}) %reduce-scatter.9.cloned.1.call-update) | async-done | bytes 1048592 | tf_op jit(solution)/shard_map/reduce_scatter | solution.py:43
  192.7 2.1 convert_element_type.67
  194.8 0.0 all-gather.6.cloned.1.call-update
  194.8 0.0 reduce-scatter.11.cloned.1.call-start
  194.9 12.6 %reduce-scatter.7.cloned.1.call-done = f32[512,128]{1,0:T(8,128)} async-done(((f32[1024,128]{1,0:T(8,128)}), f32[512,128]{1,0:T(8,128)}) %reduce-scatter.7.cloned.1.call-update) | async-done | bytes 262160 | tf_op jit(solution)/shard_map/reduce_scatter | solution.py:40
  207.5 1.0 convert_element_type.65
  208.5 5.8 %all_gather.21 = bf16[1024,128]{1,0:T(8,128)(2,1)S(1)} all-gather(bf16[512,128]{1,0:T(8,128)(2,1)S(1)} %convert_element_type.65), channel_id=1, replica_groups=mesh['col'=2,'row'=8] {'col'}, dimensions={0}, use_global_device_ids=true | all-gather | bytes 393216 | tf_op jit(solution)/shard_map/all_gather | solution.py:41
  214.3 28.0 %all-gather.6.cloned.1.call-done = bf16[16384,128]{1,0:T(8,128)(2,1)} async-done(((bf16[2048,128]{1,0:T(8,128)(2,1)}), bf16[16384,128]{1,0:T(8,128)(2,1)}) %all-gather.6.cloned.1.call-update) | async-done | bytes 4194320 | tf_op jit(solution)/shard_map/all_gather | solution.py:38
  242.4 16.9 %fusion.4 = f32[1024,128]{1,0:T(8,128)} fusion(bf16[1024,16384]{1,0:T(8,128)(2,1)} %multiply_convert_fusion, bf16[16384,128]{1,0:T(8,128)(2,1)} %all-gather.6.cloned.1.call-done), kind=kOutput, calls=%fused_computation.14 | convolution fusion | flops 4294967296 | bytes 38273024 | tf_op jit(solution)/shard_map/dot_general | solution.py:39
  259.3 0.0 reduce-scatter.11.cloned.1.call-update
  259.3 0.0 reduce-scatter.13.cloned.1.call-start
  259.4 17.1 %fusion.5 = f32[16384,128]{1,0:T(8,128)} fusion(bf16[1024,16384]{1,0:T(8,128)(2,1)} %multiply_convert_fusion, bf16[1024,128]{1,0:T(8,128)(2,1)S(1)} %all_gather.21), kind=kOutput, calls=%fused_computation.15 | convolution fusion | flops 4294967296 | bytes 42205184 | tf_op jit(solution)/shard_map/dot_general | solution.py:42
  276.5 0.0 reduce-scatter.13.cloned.1.call-update
  276.5 0.0 reduce-scatter.17.cloned.1.call-start
  276.5 0.0 reduce-scatter.11.cloned.1.call-done
  276.6 1.1 convert_element_type.68
  277.6 6.5 %all_gather.23 = bf16[1024,128]{1,0:T(8,128)(2,1)S(1)} all-gather(bf16[512,128]{1,0:T(8,128)(2,1)S(1)} %convert_element_type.68), channel_id=1, replica_groups=mesh['col'=2,'row'=8] {'col'}, dimensions={0}, use_global_device_ids=true | all-gather | bytes 393216 | tf_op jit(solution)/shard_map/all_gather | solution.py:41
  284.2 17.2 %fusion.7 = f32[16384,128]{1,0:T(8,128)} fusion(bf16[1024,16384]{1,0:T(8,128)(2,1)} %multiply_convert_fusion, bf16[1024,128]{1,0:T(8,128)(2,1)S(1)} %all_gather.23), kind=kOutput, calls=%fused_computation.17 | convolution fusion | flops 4294967296 | bytes 42205184 | tf_op jit(solution)/shard_map/dot_general | solution.py:42
  301.4 0.0 reduce-scatter.17.cloned.1.call-update
  301.4 0.0 all-gather.8.cloned.1.call-start
  301.4 40.2 %reduce-scatter.13.cloned.1.call-done = f32[2048,128]{1,0:T(8,128)} async-done(((f32[16384,128]{1,0:T(8,128)}), f32[2048,128]{1,0:T(8,128)}) %reduce-scatter.13.cloned.1.call-update) | async-done | bytes 1048592 | tf_op jit(solution)/shard_map/reduce_scatter | solution.py:43
  341.6 69.0 %reduce-scatter.17.cloned.1.call-done = f32[2048,128]{1,0:T(8,128)} async-done(((f32[16384,128]{1,0:T(8,128)}), f32[2048,128]{1,0:T(8,128)}) %reduce-scatter.17.cloned.1.call-update) | async-done | bytes 1048592 | tf_op jit(solution)/shard_map/reduce_scatter | solution.py:43
  410.6 0.0 copy-done.1
  410.6 0.0 copy-done.3
  410.6 2.6 multiply_convert_fusion.1
  413.2 0.0 all-gather.8.cloned.1.call-update
  413.2 0.0 reduce-scatter.15.cloned.1.call-start
  413.3 32.7 %all-gather.8.cloned.1.call-done = bf16[16384,128]{1,0:T(8,128)(2,1)} async-done(((bf16[2048,128]{1,0:T(8,128)(2,1)}), bf16[16384,128]{1,0:T(8,128)(2,1)}) %all-gather.8.cloned.1.call-update) | async-done | bytes 4194320 | tf_op jit(solution)/shard_map/all_gather | solution.py:38
  445.9 16.9 %fusion.6 = f32[1024,128]{1,0:T(8,128)} fusion(bf16[1024,16384]{1,0:T(8,128)(2,1)} %multiply_convert_fusion, bf16[16384,128]{1,0:T(8,128)(2,1)} %all-gather.8.cloned.1.call-done), kind=kOutput, calls=%fused_computation.16 | convolution fusion | flops 4294967296 | bytes 38273024 | tf_op jit(solution)/shard_map/dot_general | solution.py:39
  462.9 0.0 reduce-scatter.15.cloned.1.call-update
  462.9 0.0 all-reduce.5.cloned.1.call-start
  462.9 0.0 copy-done.7
  463.0 12.7 %reduce-scatter.15.cloned.1.call-done = f32[512,128]{1,0:T(8,128)} async-done(((f32[1024,128]{1,0:T(8,128)}), f32[512,128]{1,0:T(8,128)}) %reduce-scatter.15.cloned.1.call-update) | async-done | bytes 262160 | tf_op jit(solution)/shard_map/reduce_scatter | solution.py:40
  475.7 0.0 copy-done.4
  475.7 0.0 copy-done.5
  475.7 1.0 multiply_convert_fusion.2
  476.7 0.0 copy-start
  476.7 3.2 gather_fusion
  479.9 1.0 select_select_fusion
  481.0 0.0 all-reduce.5.cloned.1.call-update
  481.0 65.5 %all-reduce.5.cloned.1.call-done = bf16[1024,128]{1,0:T(8,128)(2,1)} async-done(((bf16[1024,128]{1,0:T(8,128)(2,1)}), bf16[1024,128]{1,0:T(8,128)(2,1)}) %all-reduce.5.cloned.1.call-update) | async-done | bytes 262160 | tf_op jit(solution)/shard_map/psum | solution.py:23
  546.5 5.6 %fusion.8 = f32[1024,2048]{1,0:T(8,128)} fusion(bf16[1024,128]{1,0:T(8,128)(2,1)} %all-reduce.5.cloned.1.call-done, bf16[2048,128]{1,0:T(8,128)(2,1)S(1)} %get-tuple-element.5), kind=kOutput, calls=%fused_computation.18 | convolution fusion | flops 536870912 | bytes 9175040 | tf_op jit(solution)/shard_map/dot_general | solution.py:24
  552.1 0.0 copy-done.2
  552.1 0.0 copy-done
  (9 shorter events, 0.0 us)
Async XLA Ops:
  7.2 27.9 %copy-start.6 = (bf16[512,128]{1,0:T(8,128)(2,1)S(1)}, bf16[512,128]{1,0:T(8,128)(2,1)}, u32[]{:S(2)}) copy-start(bf16[512,128]{1,0:T(8,128)(2,1)} %param.5) | copy-start | bytes 393220
  7.2 70.1 %all-reduce.3.cloned.1.call-start = ((), (), s32[]{:S(2)}) async-start(), calls=%async_computation.6 | async-start | bytes 131072 | tf_op jit(solution)/shard_map/psum | solution.py:11
  28.7 99.5 %all-gather.4.cloned.1.call-start = ((), (), s32[]{:S(2)}) async-start(), calls=%async_computation.7 | async-start | bytes 4718592 | tf_op jit(solution)/shard_map/all_gather | solution.py:38
  29.5 163.3 %reduce-scatter.9.cloned.1.call-start = ((), (), s32[]{:S(2)}) async-start(), calls=%async_computation.9 | async-start | bytes 9437184 | tf_op jit(solution)/shard_map/reduce_scatter | solution.py:43
  128.2 79.3 %reduce-scatter.7.cloned.1.call-start = ((), (), s32[]{:S(2)}) async-start(), calls=%async_computation.8 | async-start | bytes 786432 | tf_op jit(solution)/shard_map/reduce_scatter | solution.py:40
  145.2 97.2 %all-gather.6.cloned.1.call-start = ((), (), s32[]{:S(2)}) async-start(), calls=%async_computation.10 | async-start | bytes 4718592 | tf_op jit(solution)/shard_map/all_gather | solution.py:38
  194.8 81.7 %reduce-scatter.11.cloned.1.call-start = ((), (), s32[]{:S(2)}) async-start(), calls=%async_computation.11 | async-start | bytes 786432 | tf_op jit(solution)/shard_map/reduce_scatter | solution.py:40
  259.3 82.3 %reduce-scatter.13.cloned.1.call-start = ((), (), s32[]{:S(2)}) async-start(), calls=%async_computation.12 | async-start | bytes 9437184 | tf_op jit(solution)/shard_map/reduce_scatter | solution.py:43
  276.5 134.2 %copy-start.1 = (f32[2048,128]{1,0:T(8,128)S(1)}, f32[2048,128]{1,0:T(8,128)}, u32[]{:S(2)}) copy-start(f32[2048,128]{1,0:T(8,128)} %reduce-scatter.9.cloned.1.call-done) | copy-start | bytes 3145732
  276.5 134.2 %copy-start.3 = (bf16[2048,128]{1,0:T(8,128)(2,1)S(1)}, bf16[2048,128]{1,0:T(8,128)(2,1)}, u32[]{:S(2)}) copy-start(bf16[2048,128]{1,0:T(8,128)(2,1)} %param.6) | copy-start | bytes 1572868
  276.5 134.1 %reduce-scatter.17.cloned.1.call-start = ((), (), s32[]{:S(2)}) async-start(), calls=%async_computation.15 | async-start | bytes 9437184 | tf_op jit(solution)/shard_map/reduce_scatter | solution.py:43
  301.4 161.6 %copy-start.7 = (s32[1024]{0:T(1024)S(1)}, s32[1024]{0:T(1024)}, u32[]{:S(2)}) copy-start(s32[1024]{0:T(1024)} %param.7) | copy-start | bytes 12292
  301.4 174.3 %copy-start.4 = (f32[512,128]{1,0:T(8,128)S(1)}, f32[512,128]{1,0:T(8,128)}, u32[]{:S(2)}) copy-start(f32[512,128]{1,0:T(8,128)} %reduce-scatter.7.cloned.1.call-done) | copy-start | bytes 786436
  301.4 174.3 %copy-start.5 = (f32[512,128]{1,0:T(8,128)S(1)}, f32[512,128]{1,0:T(8,128)}, u32[]{:S(2)}) copy-start(f32[512,128]{1,0:T(8,128)} %reduce-scatter.11.cloned.1.call-done) | copy-start | bytes 786436
  301.4 144.5 %all-gather.8.cloned.1.call-start = ((), (), s32[]{:S(2)}) async-start(), calls=%async_computation.13 | async-start | bytes 4718592 | tf_op jit(solution)/shard_map/all_gather | solution.py:38
  413.2 138.9 %copy-start.2 = (bf16[2048,128]{1,0:T(8,128)(2,1)}, bf16[2048,128]{1,0:T(8,128)(2,1)S(1)}, u32[]{:S(2)}) copy-start(bf16[2048,128]{1,0:T(8,128)(2,1)S(1)} %get-tuple-element.5) | copy-start | bytes 1572868
  413.2 62.5 %reduce-scatter.15.cloned.1.call-start = ((), (), s32[]{:S(2)}) async-start(), calls=%async_computation.14 | async-start | bytes 786432 | tf_op jit(solution)/shard_map/reduce_scatter | solution.py:40
  462.9 83.6 %all-reduce.5.cloned.1.call-start = ((), (), s32[]{:S(2)}) async-start(), calls=%async_computation.16 | async-start | bytes 524288 | tf_op jit(solution)/shard_map/psum | solution.py:23
  476.7 75.4 %copy-start = (bf16[512,128]{1,0:T(8,128)(2,1)}, bf16[512,128]{1,0:T(8,128)(2,1)S(1)}, u32[]{:S(2)}) copy-start(bf16[512,128]{1,0:T(8,128)(2,1)S(1)} %multiply_convert_fusion.2) | copy-start | bytes 393220
Sparse Core Ops, SparseCore 0:
  28.8 48.3 all-reduce.2
  79.1 31.9 all-gather.3
  128.3 64.4 reduce-scatter.8
  194.8 12.6 reduce-scatter.6
  209.8 32.5 all-gather.5
  259.4 12.6 reduce-scatter.10
  276.6 64.9 reduce-scatter.12
  345.6 64.9 reduce-scatter.16
  413.3 32.5 all-gather.7
  463.0 12.6 reduce-scatter.14
  481.1 65.2 all-reduce.4
where the time goes:
time: 559 us
  waiting for transfers between devices  346 us (62%)
  matrix products  108 us (19%)
  other arithmetic  64 us (11%)
  blocking collectives  23.6 us (4%)
  between operations  14 us (3%)
    reduce_scatter x3, waiting for transfers between devices, device_step(): lax.psum_scatter(item_part, 'row', scatter_dimension=0, tiled=True)  157 us
    psum x1, waiting for transfers between devices, query_scores(): picked = lax.psum(picked, ('row', 'col'))  65.5 us
    all_gather x3, waiting for transfers between devices, device_step(): item_panel = lax.all_gather(item_cur, 'row', axis=0, tiled=True)  60.7 us
    dot_general x3, matrix products, device_step(): lax.dot_general(norm_adj, user_panel, contract_rows, preferred_element_ty...  51.4 us
    dot_general x3, matrix products, device_step(): jnp.dot(norm_adj, item_panel, preferred_element_type=jnp.float32)  50.8 us
    psum x1, waiting for transfers between devices, norm_block(): deg_item = lax.psum(jnp.sum(mask_blk, axis=0), 'row')  36.5 us
    convert_element_type x1, other arithmetic, norm_block(): (inv_user[:, None] * mask_blk.astype(jnp.float32) * inv_item[None, :]).as...  32.9 us
    reduce_scatter x3, waiting for transfers between devices, device_step(): lax.psum_scatter(user_part, 'col', scatter_dimension=0, tiled=True)  25.3 us
  transfers between devices with their start and end apart: 11, of which 9 were waited for; matrix products, arithmetic and copies ran while one was open for 19% of the time, Pallas kernels for 0%

commit v1 on v0

v1 whole, which is shorter than its diff:
```python
import functools

import jax
import jax.numpy as jnp
from jax import lax
from jax.experimental import pallas as pl
from jax.experimental.pallas import tpu as pltpu
from jax.sharding import PartitionSpec as P

LAYERS = 3
BF = jnp.bfloat16
F32 = jnp.float32
EMB = 128
ROWS = 1024
STRIPE = 2048
CHIPS = 4
COLS = STRIPE * CHIPS
UROWS = 512
HALF = STRIPE // 2
NCH = 4
CH = HALF // NCH
LROWS = 128
NLOAD = 6
NSTAGE = 3
QUERIES = 1024


def al(v, m):
    return pl.multiple_of(v, m)


def dot(a, b, ca, cb):
    return lax.dot_general(a, b, (((ca,), (cb,)), ((), ())), preferred_element_type=F32)


def kernel(mask_ref, ue_ref, ie_ref, q_ref, fu_ref, fi_ref, pk_ref,
           a, part, r1, r2, panel, eut, upart, ursib, urz, invi, mbuf, stage,
           cs, csr, dus, dur, dis, dir_, usum, pkc, pks, pkz, pkx, pka,
           lsem, xs, xr, s1s, s1r, s2s, s2r, ags, agr, fws, fwr,
           usibs, usibr, uzs, uzr, uas, uar, eis, eir, dgs, dgr, pqs, pqr):
    row = lax.axis_index('row')
    z = lax.axis_index('col')
    c = lax.rem(row, 2)
    x = lax.rem(lax.div(row, 2), 2)
    y = lax.div(row, 4)
    me = y * 2 + x

    def dev(xx, yy, cc, zz):
        return {'row': (yy * 2 + xx) * 2 + cc, 'col': zz}

    ox, oy, oc, oz = 1 - x, 1 - y, 1 - c, 1 - z
    xn, yn, dg = dev(ox, y, c, z), dev(x, oy, c, z), dev(ox, oy, c, z)
    zn, sib, zsib = dev(x, y, c, oz), dev(x, y, oc, z), dev(x, y, oc, oz)

    def rcopy(src, dst, ss, rs, to):
        return pltpu.make_async_remote_copy(src_ref=src, dst_ref=dst, send_sem=ss, recv_sem=rs,
                                            device_id=to, device_id_type=pl.DeviceIdType.MESH)

    barrier = pltpu.get_barrier_semaphore()
    for peer in (xn, yn, dg, zn, sib, zsib):
        pl.semaphore_signal(barrier, inc=1, device_id=peer, device_id_type=pl.DeviceIdType.MESH)

    def load(n):
        rg = lax.div(n, 8)
        p = lax.div(lax.rem(n, 8), 2)
        par = lax.rem(n, 2)
        s = 2 * p + par * c + (1 - par) * oc
        slot = lax.rem(n, NLOAD)
        return pltpu.make_async_copy(
            mask_ref.at[pl.ds(al(rg * LROWS, LROWS), LROWS), pl.ds(al(s * STRIPE, STRIPE), STRIPE)],
            mbuf.at[slot], lsem.at[slot])

    n_load = (ROWS // LROWS) * 8
    for n in range(NLOAD):
        load(n).start()

    ucol = al(c * ROWS + z * UROWS, UROWS)
    usum[...] = ue_ref[...].astype(F32)
    eut[0, :, pl.ds(ucol, UROWS)] = ue_ref[...].astype(F32).T.astype(BF)
    panel[0, pl.ds(al(me * STRIPE, STRIPE), STRIPE), :] = ie_ref[...]
    cs[...] = jnp.zeros_like(cs)
    upart[pl.ds(0, ROWS), :] = jnp.zeros((ROWS, EMB), F32)
    pl.semaphore_wait(barrier, 6)

    own_rows = pl.ds(al(me * STRIPE, STRIPE), STRIPE)

    def ei0(i):
        return rcopy(ie_ref, panel.at[0, own_rows], eis.at[i], eir.at[i], (xn, yn, dg)[i])

    def ua(j, i):
        blk = eut.at[j, :, pl.ds(ucol, UROWS)]
        return rcopy(blk, blk, uas.at[j, i], uar.at[j, i], (zn, sib, zsib)[i])

    for i in range(3):
        ei0(i).start()
    for i in range(3):
        ua(0, i).start()

    def xcopy(m):
        rg = lax.div(m, CHIPS)
        p = lax.rem(m, CHIPS)
        slot = lax.rem(m, NSTAGE)
        return rcopy(stage.at[slot],
                     a.at[pl.ds(al(c * ROWS + rg * LROWS, LROWS), LROWS), pl.ds(al(p * STRIPE, STRIPE), STRIPE)],
                     xs.at[slot], xr, sib)

    def count(m, par):
        n = 2 * m + par
        rg = lax.div(m, CHIPS)
        p = lax.rem(m, CHIPS)
        slot = lax.rem(n, NLOAD)
        sslot = lax.rem(m, NSTAGE)
        load(n).wait()
        cols = pl.ds(al(p * STRIPE, STRIPE), STRIPE)
        acc = jnp.zeros((8, STRIPE), F32)
        for g in range(LROWS // 16):
            v = mbuf[slot, g * 16:(g + 1) * 16, :].astype(F32)
            b = v.astype(BF)
            if par == 0:
                stage[sslot, g * 16:(g + 1) * 16, :] = b
            else:
                a[pl.ds(al(c * ROWS + rg * LROWS + g * 16, 16), 16), cols] = b
            acc = acc + v[0:8] + v[8:16]
            parts = [v[:, i * 128:(i + 1) * 128] for i in range(STRIPE // 128)]
            while len(parts) > 1:
                parts = [parts[i] + parts[i + 1] for i in range(0, len(parts), 2)]
            rsl = pl.ds(al(rg * LROWS + g * 16, 16), 16)
            upart[rsl, :] = upart[rsl, :] + parts[0]
        cs[par, :, cols] = cs[par, :, cols] + acc

        @pl.when(n + NLOAD < n_load)
        def _():
            load(n + NLOAD).start()

    def mask_step(m, _):
        @pl.when(m >= NSTAGE)
        def _():
            xcopy(m - NSTAGE).wait_send()
        count(m, 0)
        xcopy(m).start()
        count(m, 1)
        return 0

    n_pairs = n_load // 2
    lax.fori_loop(0, n_pairs, mask_step, 0)

    def csend():
        return rcopy(cs.at[0], csr, dgs.at[6], dgr.at[6], sib)

    def dusend(i):
        return rcopy(dus, dur.at[i], dgs.at[i], dgr.at[i], (zn, sib, zsib)[i])

    def disend(i):
        return rcopy(dis, dir_.at[i], dgs.at[3 + i], dgr.at[3 + i], (xn, yn, dg)[i])

    csend().start()
    for b in range(ROWS // 128):
        t = upart[b * 128:(b + 1) * 128, :].T
        v = jnp.sum(t, axis=0, keepdims=True)
        dus[:, b * 128:(b + 1) * 128] = jnp.broadcast_to(v, (8, 128))
    for i in range(3):
        dusend(i).start()
    csend().wait_recv()
    tot = jnp.sum(cs[1] + csr[...], axis=0, keepdims=True)
    for g in range(8):
        dis[g:g + 1, :] = tot[:, g * 1024:(g + 1) * 1024]
    for i in range(3):
        disend(i).start()
    for m in range(n_pairs - NSTAGE, n_pairs):
        xcopy(m).wait_send()
    for i in range(3):
        dusend(i).wait_recv()
    for blk, v in ((c, dus[...] + dur[0]), (oc, dur[1] + dur[2])):
        v = lax.rsqrt(jnp.maximum(v, 1.0))
        for b in range(ROWS // 128):
            w = jnp.broadcast_to(v[0:1, b * 128:(b + 1) * 128], (128, 128))
            upart[pl.ds(al(blk * ROWS + b * 128, 128), 128), :] = w.T
    for i in range(3):
        disend(i).wait_recv()
    v = lax.rsqrt(jnp.maximum((dis[...] + dir_[0]) + (dir_[1] + dir_[2]), 1.0))
    for g in range(8):
        invi[0:1, g * 1024:(g + 1) * 1024] = v[g:g + 1, :]
    half_a = a.at[pl.ds(al(oc * ROWS, ROWS), ROWS), :]
    rcopy(half_a, half_a, xs.at[0], xr, sib).wait_recv()
    for i in range(3):
        dusend(i).wait_send()
        disend(i).wait_send()
    csend().wait_send()

    def s1(st, t, k):
        h = lax.rem(t, 2)
        to = dev(x + (1 - h) * (1 - 2 * x), y + h * (1 - 2 * y), c, z)
        return rcopy(part.at[t, k], r1.at[st, t, k], s1s.at[st, t, k], s1r.at[st, t, k], to)

    def s2(st, h, k):
        return rcopy(part.at[6 + h, k], r2.at[st, h, k], s2s.at[st, h, k], s2r.at[st, h, k], (yn, xn)[h])

    def chunk_rows(q, h, k):
        return pl.ds(al(q * STRIPE + h * HALF + k * CH, CH), CH)

    def ag(st, d, h, k):
        blk = panel.at[1 - st, chunk_rows(me, h, k)]
        return rcopy(blk, blk, ags.at[st, d, h, k], agr.at[st, d, h, k], (xn, yn)[d])

    def fw(st, h, k):
        q = (y * 2 + ox, oy * 2 + x)[h]
        blk = panel.at[1 - st, chunk_rows(q, h, k)]
        return rcopy(blk, blk, fws.at[st, h, k], fwr.at[st, h, k], (yn, xn)[h])

    def usib(st):
        return rcopy(upart.at[pl.ds(al(oc * ROWS, ROWS), ROWS)], ursib.at[st], usibs.at[st], usibr.at[st], sib)

    def uz(st):
        return rcopy(upart.at[pl.ds(al(c * ROWS + oz * UROWS, UROWS), UROWS)], urz.at[st],
                     uzs.at[st], uzr.at[st], zn)

    qh, qq = QUERIES // 2, QUERIES // 4
    quarter = pl.ds(al(c * qh + z * qq, qq), qq)

    def pq_sib():
        return rcopy(pkc.at[pl.ds(al(oc * qh, qh), qh)], pks, pqs.at[0], pqr.at[0], sib)

    def pq_z():
        return rcopy(pkc.at[pl.ds(al(c * qh + oz * qq, qq), qq)], pkz, pqs.at[1], pqr.at[1], zn)

    def pq_x(i):
        return rcopy(pkc.at[quarter], pkx.at[i], pqs.at[2 + i], pqr.at[2 + i], (xn, yn, dg)[i])

    def pq_a(i):
        return rcopy(pka.at[quarter], pka.at[quarter], pqs.at[5 + i], pqr.at[5 + i], (zn, sib, zsib)[i])

    def badd(u, v):
        return (u.astype(F32) + v.astype(F32)).astype(BF)

    def round_body(j, _):
        st = lax.rem(j, 2)
        last = j == LAYERS - 1
        more = j < LAYERS - 1
        for i in range(3):
            ua(j, i).wait_recv()

        def item_tile(t, _):
            h = lax.rem(t, 2)
            u = lax.div(t, 2)
            f1, f2 = 1 - lax.div(u, 2), lax.rem(u, 2)
            fx = (1 - h) * f1 + h * f2
            fy = (1 - h) * f2 + h * f1
            q = (y + fy - 2 * y * fy) * 2 + (x + fx - 2 * x * fx)
            base = al(q * STRIPE + h * HALF, HALF)

            @pl.when(j == 0)
            def _():
                def norm(g, _):
                    rsl = pl.ds(al(g * 128, 128), 128)
                    iu = upart[rsl, :]
                    for b in range(HALF // 128):
                        cc = pl.ds(al(base + b * 128, 128), 128)
                        a[rsl, cc] = a[rsl, cc] * (iu * invi[0:1, cc]).astype(BF)
                    return 0
                lax.fori_loop(0, 2 * ROWS // 128, norm, 0)

            res = dot(eut[j], a[:, pl.ds(base, HALF)], 1, 0)
            for k in range(NCH):
                part[t, k] = res[:, k * CH:(k + 1) * CH]

            @pl.when(t < 4)
            def _():
                for k in range(NCH):
                    s1(st, t, k).start()
            return 0

        lax.fori_loop(0, 8, item_tile, 0)

        @pl.when(j == 0)
        def _():
            for i in range(3):
                ei0(i).wait_recv()

        @pl.when(j > 0)
        def _():
            for k in range(NCH):
                ag(1 - st, 0, 1, k).wait_recv()
                ag(1 - st, 1, 0, k).wait_recv()
                fw(1 - st, 0, k).wait_recv()
                fw(1 - st, 1, k).wait_recv()

        def user_tile(i, _):
            b = lax.div(i, 2)
            rsl = pl.ds(al((b * c + (1 - b) * oc) * ROWS + lax.rem(i, 2) * UROWS, UROWS), UROWS)
            upart[rsl, :] = dot(a[rsl, :], panel[st], 1, 0)

            @pl.when(i == 1)
            def _():
                usib(st).start()
            return 0

        lax.fori_loop(0, 4, user_tile, 0)
        usib(st).wait_recv()
        mine = pl.ds(al(c * ROWS, ROWS), ROWS)
        upart[mine, :] = upart[mine, :] + ursib[st]
        uz(st).start()

        def stage1(k, _):
            for h in range(2):
                s1(st, 2 + h, k).wait_recv()
                part[6 + h, k] = part[6 + h, k] + r1[st, 2 + h, k]
                s1(st, h, k).wait_recv()
                part[4 + h, k] = part[4 + h, k] + r1[st, h, k]
                s2(st, h, k).start()
            return 0

        lax.fori_loop(0, NCH - 1, stage1, 0)

        uz(st).wait_recv()
        e = (upart[pl.ds(ucol, UROWS), :] + urz[st]).astype(BF).astype(F32)
        usum[...] = usum[...] + e

        @pl.when(more)
        def _():
            eut[j + 1, :, pl.ds(ucol, UROWS)] = e.T.astype(BF)
            for i in range(3):
                ua(j + 1, i).start()

        @pl.when(last)
        def _():
            fu = (usum[...] * (1.0 / (LAYERS + 1))).astype(BF)
            fu_ref[...] = fu
            ids = lax.broadcasted_iota(jnp.int32, (UROWS, QUERIES), 0) + (row * 2 + z) * UROWS
            hot = jnp.where(ids == q_ref[...], 1.0, 0.0).astype(BF)
            pkc[...] = dot(hot, fu, 0, 0).astype(BF)
            pq_sib().start()

        stage1(NCH - 1, 0)

        @pl.when(last)
        def _():
            pq_sib().wait_recv()
            hrows = pl.ds(al(c * qh, qh), qh)
            pkc[hrows, :] = badd(pkc[hrows, :], pks[...])
            pq_z().start()

        def stage2(k, _):
            for h in range(2):
                s2(st, h, k).wait_recv()
                e = (part[4 + h, k] + r2[st, h, k]).T.astype(BF)
                rsl = chunk_rows(me, h, k)

                @pl.when(more)
                def _():
                    panel[1 - st, rsl, :] = e
                    ag(st, 0, h, k).start()
                    ag(st, 1, h, k).start()

                @pl.when(last)
                def _():
                    loc = pl.ds(al(h * HALF + k * CH, CH), CH)
                    tot = ie_ref[loc, :].astype(F32) + panel[1, rsl, :].astype(F32)
                    tot = tot + panel[0, rsl, :].astype(F32) + e.astype(F32)
                    fi_ref[loc, :] = (tot * (1.0 / (LAYERS + 1))).astype(BF)
            return 0

        stage2(0, 0)

        @pl.when(last)
        def _():
            pq_z().wait_recv()
            pkc[quarter, :] = badd(pkc[quarter, :], pkz[...])
            for i in range(3):
                pq_x(i).start()

        lax.fori_loop(1, NCH, stage2, 0)

        @pl.when(more)
        def _():
            def forward(k, _):
                ag(st, 0, 0, k).wait_recv()
                fw(st, 0, k).start()
                ag(st, 1, 1, k).wait_recv()
                fw(st, 1, k).start()
                return 0
            lax.fori_loop(0, NCH, forward, 0)

        usib(st).wait_send()
        uz(st).wait_send()
        for i in range(3):
            ua(j, i).wait_send()
        for k in range(NCH):
            for t in range(4):
                s1(st, t, k).wait_send()
            for h in range(2):
                s2(st, h, k).wait_send()

        @pl.when(j > 0)
        def _():
            for k in range(NCH):
                for h in range(2):
                    ag(1 - st, 0, h, k).wait_send()
                    ag(1 - st, 1, h, k).wait_send()
                    fw(1 - st, h, k).wait_send()
        return 0

    lax.fori_loop(0, LAYERS, round_body, 0)

    for i in range(3):
        ei0(i).wait_send()
        pq_x(i).wait_recv()
    tot = badd(badd(pkc[quarter, :], pkx[0]), badd(pkx[1], pkx[2]))
    pka[quarter, :] = tot
    for i in range(3):
        pq_a(i).start()
    pq_sib().wait_send()
    pq_z().wait_send()
    for i in range(3):
        pq_x(i).wait_send()
        pq_a(i).wait_recv()
    pk_ref[...] = pka[...]
    for i in range(3):
        pq_a(i).wait_send()


def propagate(mask_blk, user_shard, item_shard, queries):
    vm = pl.BlockSpec(memory_space=pltpu.VMEM)
    dma = pltpu.SemaphoreType.DMA
    qh, qq = QUERIES // 2, QUERIES // 4
    scratch = [
        pltpu.VMEM((2 * ROWS, COLS), BF),
        pltpu.VMEM((8, NCH, EMB, CH), F32),
        pltpu.VMEM((2, 4, NCH, EMB, CH), F32),
        pltpu.VMEM((2, 2, NCH, EMB, CH), F32),
        pltpu.VMEM((2, COLS, EMB), BF),
        pltpu.VMEM((LAYERS, EMB, 2 * ROWS), BF),
        pltpu.VMEM((2 * ROWS, EMB), F32),
        pltpu.VMEM((2, ROWS, EMB), F32),
        pltpu.VMEM((2, UROWS, EMB), F32),
        pltpu.VMEM((1, COLS), F32),
        pltpu.VMEM((NLOAD, LROWS, STRIPE), jnp.int32),
        pltpu.VMEM((NSTAGE, LROWS, STRIPE), BF),
        pltpu.VMEM((2, 8, COLS), F32),
        pltpu.VMEM((8, COLS), F32),
        pltpu.VMEM((8, ROWS), F32),
        pltpu.VMEM((3, 8, ROWS), F32),
        pltpu.VMEM((8, COLS // 8), F32),
        pltpu.VMEM((3, 8, COLS // 8), F32),
        pltpu.VMEM((UROWS, EMB), F32),
        pltpu.VMEM((QUERIES, EMB), BF),
        pltpu.VMEM((qh, EMB), BF),
        pltpu.VMEM((qq, EMB), BF),
        pltpu.VMEM((3, qq, EMB), BF),
        pltpu.VMEM((QUERIES, EMB), BF),
        dma((NLOAD,)), dma((NSTAGE,)), dma,
        dma((2, 4, NCH)), dma((2, 4, NCH)),
        dma((2, 2, NCH)), dma((2, 2, NCH)),
        dma((2, 2, 2, NCH)), dma((2, 2, 2, NCH)),
        dma((2, 2, NCH)), dma((2, 2, NCH)),
        dma((2,)), dma((2,)), dma((2,)), dma((2,)),
        dma((LAYERS, 3)), dma((LAYERS, 3)),
        dma((3,)), dma((3,)), dma((7,)), dma((7,)), dma((8,)), dma((8,)),
    ]
    return pl.pallas_call(
        kernel,
        out_shape=(jax.ShapeDtypeStruct((UROWS, EMB), BF),
                   jax.ShapeDtypeStruct((STRIPE, EMB), BF),
                   jax.ShapeDtypeStruct((QUERIES, EMB), BF)),
        in_specs=[pl.BlockSpec(memory_space=pl.ANY), vm, vm, vm],
        out_specs=(vm, vm, vm),
        scratch_shapes=scratch,
        compiler_params=pltpu.CompilerParams(collective_id=0, has_side_effects=True,
                                             vmem_limit_bytes=67043328),
        name='propagate',
    )(mask_blk, user_shard, item_shard, queries)


def solution(mesh):
    def device_step(mask_blk, user_shard, item_shard, queries):
        fu, fi, picked = propagate(mask_blk, user_shard, item_shard, queries.reshape(1, QUERIES))
        scores = lax.dot_general(picked, fi, (((1,), (1,)), ((), ())), preferred_element_type=F32)
        return fu, fi, scores

    return jax.shard_map(
        device_step, mesh=mesh,
        in_specs=(P('row', 'col'), P(('row', 'col'), None), P(('col', 'row'), None), P()),
        out_specs=(P(('row', 'col'), None), P(('col', 'row'), None), P(None, ('col', 'row'))),
        check_vma=False)
```

time: 559 us -> 197 us (0.35)
  waiting for transfers between devices: 346 us -> 0 us
  Pallas kernels: 0 us -> 189 us
  matrix products: 108 us -> 5.84 us
  other arithmetic: 64 us -> 0 us
  blocking collectives: 23.6 us -> 0 us
  between operations: 14 us -> 0.66 us
    pallas_call x0 -> x1, Pallas kernels: none -> 189 us  [propagate(): pl.pallas_call(kernel, out_shape=(jax.ShapeDtypeStruct((UROWS, EMB), BF),...]
    reduce_scatter x6 -> x0, waiting for transfers between devices: 182 us -> none  [the longest x3 157 us: device_step(): lax.psum_scatter(item_part, 'row', scatter_dimension=0, tiled=True)]
    dot_general x7 -> x1, matrix products: 108 us -> 5.84 us  [device_step(): lax.dot_general(picked, fi, (((1,), (1,)), ((), ())), preferred_element_t...]
    psum x2 -> x0, waiting for transfers between devices: 102 us -> none  [the longest x1 65.5 us: query_scores(): picked = lax.psum(picked, ('row', 'col'))]
    all_gather x3 -> x0, waiting for transfers between devices: 60.7 us -> none  [device_step(): item_panel = lax.all_gather(item_cur, 'row', axis=0, tiled=True)]
    convert_element_type x6 -> x0, other arithmetic: 40.6 us -> none  [the longest x1 32.9 us: norm_block(): (inv_user[:, None] * mask_blk.astype(jnp.float32) * inv_item[None, :]).as...]
    reduce_sum x1 -> x0, other arithmetic: 21.5 us -> none  [norm_block(): deg_user = lax.psum(jnp.sum(mask_blk, axis=1), 'col')]
    all_gather x3 -> x0, blocking collectives: 18 us -> none  [device_step(): user_panel = lax.all_gather(user_cur, 'col', axis=0, tiled=True)]
  transfers between devices with their start and end apart: 11 -> 0, of which waited for: 9 -> 0; matrix products, arithmetic and copies ran while one was open for 19% -> 0% of each run, Pallas kernels for 0% -> 0%
where the time goes in v1:
time: 197 us
  Pallas kernels  189 us (96%)
  matrix products  5.84 us (3%)
    pallas_call x1, Pallas kernels, propagate(): pl.pallas_call(kernel, out_shape=(jax.ShapeDtypeStruct((UROWS, EMB), BF),...  189 us
    dot_general x1, matrix products, device_step(): lax.dot_general(picked, fi, (((1,), (1,)), ((), ())), preferred_element_t...  5.84 us

profile of v1, /device:TPU:0, one launch (start us, length us, event | category | flops | bytes accessed | tf_op | source)
XLA Modules:
  0.0 197.0 jit_solution(10009428661750886555)
XLA Ops:
  0.6 189.0 %propagate.1 = (bf16[512,128]{1,0:T(8,128)(2,1)}, bf16[2048,128]{1,0:T(8,128)(2,1)}, bf16[1024,128]{1,0:T(8,128)(2,1)}) custom-call(s32[1024,16384]{1,0:T(8,128)} %mask_ref.1, bf16[512,128]{1,0:T(8,128)(2,1)} %ue_ref.1, bf16[2048,128]{1,0:T(8,128)(2,1)} %ie_ref.1, s32[1,1024]{1,0:T(1,128)} %bitcast.3), custom_call_target="tpu_custom_call" | custom-call | tf_op jit(solution)/shard_map/propagate/pallas_call | solution.py:459
  189.7 0.0 copy-start.1
  189.7 0.0 copy-start
  189.7 5.8 %fusion = f32[1024,2048]{1,0:T(8,128)} fusion(bf16[1024,128]{1,0:T(8,128)(2,1)} %get-tuple-element.8, bf16[2048,128]{1,0:T(8,128)(2,1)} %get-tuple-element.13), kind=kOutput, calls=%fused_computation | convolution fusion | flops 536870912 | bytes 9175040 | tf_op jit(solution)/shard_map/dot_general | solution.py:476
  195.5 0.0 copy-done.1
  195.5 0.7 copy.9
  196.2 0.0 copy-done
  196.2 0.8 copy.10
Async XLA Ops:
  189.7 5.9 %copy-start.1 = (bf16[512,128]{1,0:T(8,128)(2,1)S(1)}, bf16[512,128]{1,0:T(8,128)(2,1)}, u32[]{:S(2)}) copy-start(bf16[512,128]{1,0:T(8,128)(2,1)} %get-tuple-element.12) | copy-start | bytes 393220
  189.7 6.5 %copy-start = (bf16[2048,128]{1,0:T(8,128)(2,1)S(1)}, bf16[2048,128]{1,0:T(8,128)(2,1)}, u32[]{:S(2)}) copy-start(bf16[2048,128]{1,0:T(8,128)(2,1)} %get-tuple-element.13) | copy-start | bytes 1572868

commit v2 on v1

v2 whole, which is shorter than its diff:
```python
import functools

import jax
import jax.numpy as jnp
from jax import lax
from jax.experimental import pallas as pl
from jax.experimental.pallas import tpu as pltpu
from jax.sharding import PartitionSpec as P

LAYERS = 3
BF = jnp.bfloat16
F32 = jnp.float32
EMB = 128
ROWS = 1024
STRIPE = 2048
CHIPS = 4
COLS = STRIPE * CHIPS
UROWS = 512
HALF = STRIPE // 2
NCH = 4
CH = HALF // NCH
LROWS = 128
NLOAD = 6
NSTAGE = 8
QUERIES = 1024


def al(v, m):
    return pl.multiple_of(v, m)


def dot(a, b, ca, cb):
    return lax.dot_general(a, b, (((ca,), (cb,)), ((), ())), preferred_element_type=F32)


def kernel(mask_ref, ue_ref, ie_ref, q_ref, fu_ref, fi_ref, pk_ref,
           a, part, r1, r2, panel, eut, upart, ursib, urz, invi, mbuf, stage,
           cs, dcs, dcr, dus, dur, usum, pkc, pks, pkz, pkx, pka,
           lsem, xs, xr, s1s, s1r, s2s, s2r, ags, agr, fws, fwr,
           usibs, usibr, uzs, uzr, uas, uar, eis, eir, dgs, dgr, dvs, dvr, pqs, pqr):
    row = lax.axis_index('row')
    z = lax.axis_index('col')
    c = lax.rem(row, 2)
    x = lax.rem(lax.div(row, 2), 2)
    y = lax.div(row, 4)
    me = y * 2 + x

    def dev(xx, yy, cc, zz):
        return {'row': (yy * 2 + xx) * 2 + cc, 'col': zz}

    ox, oy, oc, oz = 1 - x, 1 - y, 1 - c, 1 - z
    xn, yn, dg = dev(ox, y, c, z), dev(x, oy, c, z), dev(ox, oy, c, z)
    zn, sib, zsib = dev(x, y, c, oz), dev(x, y, oc, z), dev(x, y, oc, oz)
    xnc, ync, dgc = dev(ox, y, oc, z), dev(x, oy, oc, z), dev(ox, oy, oc, z)

    def rcopy(src, dst, ss, rs, to):
        return pltpu.make_async_remote_copy(src_ref=src, dst_ref=dst, send_sem=ss, recv_sem=rs,
                                            device_id=to, device_id_type=pl.DeviceIdType.MESH)

    barrier = pltpu.get_barrier_semaphore()
    peers = (xn, yn, dg, zn, sib, zsib, xnc, ync, dgc)
    for peer in peers:
        pl.semaphore_signal(barrier, inc=1, device_id=peer, device_id_type=pl.DeviceIdType.MESH)

    n_group = ROWS // LROWS
    n_load = n_group * 2 * CHIPS

    def stripe(i):
        fx = 1 - lax.rem(i, 2)
        fy = lax.rem(lax.div(i + 1, 2), 2)
        return (y + fy - 2 * y * fy) * 2 + (x + fx - 2 * x * fx)

    def load_at(i, rg, par, n):
        s = 2 * stripe(i) + par * c + (1 - par) * oc
        slot = lax.rem(n, NLOAD)
        return pltpu.make_async_copy(
            mask_ref.at[pl.ds(al(rg * LROWS, LROWS), LROWS), pl.ds(al(s * STRIPE, STRIPE), STRIPE)],
            mbuf.at[slot], lsem.at[slot])

    def load(n):
        first = 1 - lax.min(lax.div(n, 2 * n_group), 1)
        i = lax.div(n, 2 * n_group)
        w = lax.rem(n, 2 * n_group)
        rg = first * lax.rem(w, n_group) + (1 - first) * lax.div(w, 2)
        par = first * (1 - lax.div(w, n_group)) + (1 - first) * lax.rem(w, 2)
        return load_at(i, rg, par, n)

    for n in range(NLOAD):
        load(jnp.int32(n)).start()

    ucol = al(c * ROWS + z * UROWS, UROWS)
    usum[...] = ue_ref[...].astype(F32)
    eut[0, :, pl.ds(ucol, UROWS)] = ue_ref[...].astype(F32).T.astype(BF)
    own_rows = pl.ds(al(me * STRIPE, STRIPE), STRIPE)
    panel[0, own_rows, :] = ie_ref[...]
    cs[...] = jnp.zeros_like(cs)
    upart[pl.ds(0, ROWS), :] = jnp.zeros((ROWS, EMB), F32)

    def count(i, rg, par, n, sslot):
        p = stripe(i)
        slot = lax.rem(n, NLOAD)
        load_at(i, rg, par, n).wait()
        cols = pl.ds(al(p * STRIPE, STRIPE), STRIPE)
        acc = jnp.zeros((8, STRIPE), F32)
        for g in range(LROWS // 16):
            v = mbuf[slot, g * 16:(g + 1) * 16, :].astype(F32)
            b = v.astype(BF)
            if par == 0:
                stage[sslot, g * 16:(g + 1) * 16, :] = b
            else:
                a[pl.ds(al(c * ROWS + rg * LROWS + g * 16, 16), 16), cols] = b
            acc = acc + v[0:8] + v[8:16]
            parts = [v[:, q * 128:(q + 1) * 128] for q in range(STRIPE // 128)]
            while len(parts) > 1:
                parts = [parts[q] + parts[q + 1] for q in range(0, len(parts), 2)]
            rsl = pl.ds(al(rg * LROWS + g * 16, 16), 16)
            upart[rsl, :] = upart[rsl, :] + parts[0]
        cs[par] = cs[par] + acc

        @pl.when(n + NLOAD < n_load)
        def _():
            load(n + NLOAD).start()

    def xcopy(i, rg):
        slot = lax.rem(i * n_group + rg, NSTAGE)
        return rcopy(stage.at[slot],
                     a.at[pl.ds(al(c * ROWS + rg * LROWS, LROWS), LROWS), pl.ds(al(stripe(i) * STRIPE, STRIPE), STRIPE)],
                     xs.at[slot], xr.at[i], sib)

    def dgsend(p, i):
        return rcopy(dcs.at[(1, 1, 1, 0, 0, 0, 0)[i], p], dcr.at[i, p], dgs.at[i, p], dgr.at[i, p],
                     (xn, yn, dg, sib, xnc, ync, dgc)[i])

    def dusend(i):
        return rcopy(dus, dur.at[i], dvs.at[i], dvr.at[i], (zn, sib, zsib)[i])

    def stripe_degrees(i):
        p = stripe(i)
        for par in range(2):
            v = jnp.sum(cs[par], axis=0, keepdims=True)
            for g in range(8):
                dcs[par, p, g:g + 1, :] = v[:, g * 256:(g + 1) * 256]
        cs[...] = jnp.zeros_like(cs)
        for k in range(7):
            dgsend(p, k).start()

    def own_first(rg, _):
        count(0, rg, 1, rg, 0)
        return 0

    lax.fori_loop(0, n_group, own_first, 0)
    pl.semaphore_wait(barrier, len(peers))

    def ei0(i):
        return rcopy(ie_ref, panel.at[0, own_rows], eis.at[i], eir.at[i], (xn, yn, dg)[i])

    def ua(j, i):
        blk = eut.at[j, :, pl.ds(ucol, UROWS)]
        return rcopy(blk, blk, uas.at[j, i], uar.at[j, i], (zn, sib, zsib)[i])

    def sib_first(rg, _):
        count(0, rg, 0, n_group + rg, rg)
        xcopy(0, rg).start()
        return 0

    lax.fori_loop(0, n_group, sib_first, 0)
    for i in range(3):
        ei0(i).start()
    for i in range(3):
        ua(0, i).start()
    stripe_degrees(0)

    def mask_step(m, _):
        i = lax.div(m, n_group)
        rg = lax.rem(m, n_group)
        xcopy(i - 1, rg).wait_send()
        count(i, rg, 0, 2 * m, rg)
        xcopy(i, rg).start()
        count(i, rg, 1, 2 * m + 1, 0)

        @pl.when(i == CHIPS - 1)
        def _():
            rsl = pl.ds(al(rg * LROWS, LROWS), LROWS)
            v = jnp.sum(upart[rsl, :].T, axis=0, keepdims=True)
            dus[:, rsl] = jnp.broadcast_to(v, (8, LROWS))

        @pl.when(rg == n_group - 1)
        def _():
            stripe_degrees(i)
        return 0

    lax.fori_loop(n_group, CHIPS * n_group, mask_step, 0)

    for i in range(3):
        dusend(i).start()

    def stripe_inverse(i):
        p = stripe(i)
        for k in range(7):
            dgsend(p, k).wait_recv()
        v = dcs[1, p]
        for k in range(7):
            v = v + dcr[k, p]
        v = lax.rsqrt(jnp.maximum(v, 1.0))
        for g in range(8):
            invi[0:1, pl.ds(al(p * STRIPE + g * 256, 256), 256)] = v[g:g + 1, :]

    def swapped(i):
        region = a.at[pl.ds(al(oc * ROWS, ROWS), ROWS), pl.ds(al(stripe(i) * STRIPE, STRIPE), STRIPE)]
        rcopy(region, region, xs.at[0], xr.at[i], sib).wait_recv()

    for i in range(3):
        stripe_inverse(i)
    for i in range(3):
        dusend(i).wait_recv()
    for blk, v in ((c, dus[...] + dur[0]), (oc, dur[1] + dur[2])):
        v = lax.rsqrt(jnp.maximum(v, 1.0))
        for b in range(ROWS // 128):
            w = jnp.broadcast_to(v[0:1, b * 128:(b + 1) * 128], (128, 128))
            upart[pl.ds(al(blk * ROWS + b * 128, 128), 128), :] = w.T
    for i in range(3):
        swapped(i)

    def tile_q(t):
        h = lax.rem(t, 2)
        u = lax.div(t, 2)
        f1, f2 = 1 - lax.div(u, 2), lax.rem(lax.div(u + 1, 2), 2)
        fx = (1 - h) * f1 + h * f2
        fy = (1 - h) * f2 + h * f1
        return (y + fy - 2 * y * fy) * 2 + (x + fx - 2 * x * fx)

    def s1(st, t, k):
        h = lax.rem(t, 2)
        to = dev(x + (1 - h) * (1 - 2 * x), y + h * (1 - 2 * y), c, z)
        return rcopy(part.at[t, k], r1.at[t, k], s1s.at[st, t, k], s1r.at[st, t, k], to)

    def s2(st, h, k):
        return rcopy(part.at[4 + h, k], r2.at[h, k], s2s.at[st, h, k], s2r.at[st, h, k], (yn, xn)[h])

    def chunk_rows(q, h, k):
        return pl.ds(al(q * STRIPE + h * HALF + k * CH, CH), CH)

    def ag(st, d, h, k):
        blk = panel.at[1 - st, chunk_rows(me, h, k)]
        return rcopy(blk, blk, ags.at[st, d, h, k], agr.at[st, d, h, k], (xn, yn)[d])

    def fw(st, h, k):
        q = (y * 2 + ox, oy * 2 + x)[h]
        blk = panel.at[1 - st, chunk_rows(q, h, k)]
        return rcopy(blk, blk, fws.at[st, h, k], fwr.at[st, h, k], (yn, xn)[h])

    def usib(j):
        return rcopy(upart.at[pl.ds(al(oc * ROWS, ROWS), ROWS)], ursib, usibs.at[j], usibr.at[j], sib)

    def uz(j):
        return rcopy(upart.at[pl.ds(al(c * ROWS + oz * UROWS, UROWS), UROWS)], urz,
                     uzs.at[j], uzr.at[j], zn)

    qh, qq = QUERIES // 2, QUERIES // 4
    quarter = pl.ds(al(c * qh + z * qq, qq), qq)

    def pq_sib():
        return rcopy(pkc.at[pl.ds(al(oc * qh, qh), qh)], pks, pqs.at[0], pqr.at[0], sib)

    def pq_z():
        return rcopy(pkc.at[pl.ds(al(c * qh + oz * qq, qq), qq)], pkz, pqs.at[1], pqr.at[1], zn)

    def pq_x(i):
        return rcopy(pkc.at[quarter], pkx.at[i], pqs.at[2 + i], pqr.at[2 + i], (xn, yn, dg)[i])

    def pq_a(i):
        return rcopy(pka.at[quarter], pka.at[quarter], pqs.at[5 + i], pqr.at[5 + i], (zn, sib, zsib)[i])

    def badd(u, v):
        return (u.astype(F32) + v.astype(F32)).astype(BF)

    def normalise(base, width):
        def norm(g, _):
            rsl = pl.ds(al(g * 128, 128), 128)
            iu = upart[rsl, :]
            for b in range(width // 128):
                cc = pl.ds(al(base + b * 128, 128), 128)
                a[rsl, cc] = a[rsl, cc] * (iu * invi[0:1, cc]).astype(BF)
            return 0
        lax.fori_loop(0, 2 * ROWS // 128, norm, 0)

    for j in range(LAYERS):
        st = j % 2
        last = j == LAYERS - 1
        for i in range(3):
            ua(j, i).wait_recv()

        def item_tile(t, _):
            base = al(tile_q(t) * STRIPE + lax.rem(t, 2) * HALF, HALF)
            if j == 0:
                normalise(base, HALF)
            res = dot(eut[j], a[:, pl.ds(base, HALF)], 1, 0)
            for k in range(NCH):
                part[t, k] = res[:, k * CH:(k + 1) * CH]
            return 0

        def send_tile(t, _):
            item_tile(t, 0)
            for k in range(NCH):
                s1(st, t, k).start()
            return 0

        def first_chunk(n, _):
            t = lax.rem(n, 2)
            k = lax.div(n, 2)
            base = al(tile_q(t) * STRIPE + t * HALF + k * CH, CH)
            normalise(base, CH)
            part[t, k] = dot(eut[j], a[:, pl.ds(base, CH)], 1, 0)
            s1(st, t, k).start()
            return 0

        def stage1(k, _):
            for h in range(2):
                s1(st, 2 + h, k).wait_recv()
                part[4 + h, k] = part[4 + h, k] + r1[2 + h, k]
                s1(st, h, k).wait_recv()
                part[6 + h, k] = part[6 + h, k] + r1[h, k]
                s2(st, h, k).start()
            return 0

        def stage2(k, _):
            for h in range(2):
                s2(st, h, k).wait_recv()
                e = (part[6 + h, k] + r2[h, k]).T.astype(BF)
                rsl = chunk_rows(me, h, k)
                if last:
                    loc = pl.ds(al(h * HALF + k * CH, CH), CH)
                    tot = ie_ref[loc, :].astype(F32) + panel[1, rsl, :].astype(F32)
                    tot = tot + panel[0, rsl, :].astype(F32) + e.astype(F32)
                    fi_ref[loc, :] = (tot * (1.0 / (LAYERS + 1))).astype(BF)
                else:
                    panel[1 - st, rsl, :] = e
                    ag(st, 0, h, k).start()
                    ag(st, 1, h, k).start()
            return 0

        def forward(k, _):
            ag(st, 0, 0, k).wait_recv()
            fw(st, 0, k).start()
            ag(st, 1, 1, k).wait_recv()
            fw(st, 1, k).start()
            return 0

        def user_near(i, _):
            rsl = pl.ds(al(i * UROWS, UROWS), UROWS)
            tot = None
            for q in (me, y * 2 + ox, oy * 2 + x):
                ks = pl.ds(al(q * STRIPE, STRIPE), STRIPE)
                d = dot(a[rsl, ks], panel[st, ks, :], 1, 0)
                tot = d if tot is None else tot + d
            upart[rsl, :] = tot
            return 0

        def user_far(i, _):
            b = lax.div(i, 2)
            rsl = pl.ds(al((b * c + (1 - b) * oc) * ROWS + lax.rem(i, 2) * UROWS, UROWS), UROWS)
            ks = pl.ds(al((oy * 2 + ox) * STRIPE, STRIPE), STRIPE)
            upart[rsl, :] = upart[rsl, :] + dot(a[rsl, ks], panel[st, ks, :], 1, 0)

            @pl.when(i == 1)
            def _():
                usib(j).start()
            return 0

        def users():
            if j == 0:
                for i in range(3):
                    ei0(i).wait_recv()
            else:
                for k in range(NCH):
                    ag(1 - st, 0, 1, k).wait_recv()
                    ag(1 - st, 1, 0, k).wait_recv()
            lax.fori_loop(0, 4, user_near, 0)
            if j > 0:
                for k in range(NCH):
                    fw(1 - st, 0, k).wait_recv()
                    fw(1 - st, 1, k).wait_recv()
            lax.fori_loop(0, 4, user_far, 0)
            usib(j).wait_recv()
            mine = pl.ds(al(c * ROWS, ROWS), ROWS)
            upart[mine, :] = upart[mine, :] + ursib[...]
            uz(j).start()

        def user_final():
            uz(j).wait_recv()
            e = (upart[pl.ds(ucol, UROWS), :] + urz[...]).astype(BF).astype(F32)
            usum[...] = usum[...] + e
            if not last:
                eut[j + 1, :, pl.ds(ucol, UROWS)] = e.T.astype(BF)
                for i in range(3):
                    ua(j + 1, i).start()
                return
            fu = (usum[...] * (1.0 / (LAYERS + 1))).astype(BF)
            fu_ref[...] = fu
            ids = lax.broadcasted_iota(jnp.int32, (UROWS, QUERIES), 0) + (row * 2 + z) * UROWS
            hot = jnp.where(ids == q_ref[...], 1.0, 0.0).astype(BF)
            pkc[...] = dot(hot, fu, 0, 0).astype(BF)
            pq_sib().start()

        if j == 0:
            lax.fori_loop(0, 2 * NCH, first_chunk, 0)
            lax.fori_loop(2, 4, send_tile, 0)
            lax.fori_loop(4, 6, item_tile, 0)
            swapped(3)
            stripe_inverse(3)
            lax.fori_loop(6, 8, item_tile, 0)
            lax.fori_loop(0, NCH - 1, stage1, 0)
            users()
            stage1(NCH - 1, 0)
            lax.fori_loop(0, NCH, stage2, 0)
            user_final()
        else:
            lax.fori_loop(0, 4, send_tile, 0)
            users()
            lax.fori_loop(4, 8, item_tile, 0)
            lax.fori_loop(0, 2, stage1, 0)
            user_final()
            if last:
                pq_sib().wait_recv()
                hrows = pl.ds(al(c * qh, qh), qh)
                pkc[hrows, :] = badd(pkc[hrows, :], pks[...])
                pq_z().start()
                pq_z().wait_recv()
                pkc[quarter, :] = badd(pkc[quarter, :], pkz[...])
                for i in range(3):
                    pq_x(i).start()
            lax.fori_loop(2, NCH, stage1, 0)
            lax.fori_loop(0, NCH - 1, stage2, 0)
            if last:
                for i in range(3):
                    pq_x(i).wait_recv()
                pka[quarter, :] = badd(badd(pkc[quarter, :], pkx[0]), badd(pkx[1], pkx[2]))
                for i in range(3):
                    pq_a(i).start()
            stage2(NCH - 1, 0)
        if not last:
            lax.fori_loop(0, NCH, forward, 0)

        usib(j).wait_send()
        uz(j).wait_send()
        for i in range(3):
            ua(j, i).wait_send()
        for k in range(NCH):
            for t in range(4):
                s1(st, t, k).wait_send()
            for h in range(2):
                s2(st, h, k).wait_send()
        if j == 0:
            def drain_degrees(p, _):
                for k in range(7):
                    dgsend(p, k).wait_send()
                return 0
            lax.fori_loop(0, CHIPS, drain_degrees, 0)

            def drain_swap(rg, _):
                xcopy(CHIPS - 1, rg).wait_send()
                return 0
            lax.fori_loop(0, n_group, drain_swap, 0)
            for i in range(3):
                dusend(i).wait_send()
                ei0(i).wait_send()
        else:
            for k in range(NCH):
                for h in range(2):
                    ag(1 - st, 0, h, k).wait_send()
                    ag(1 - st, 1, h, k).wait_send()
                    fw(1 - st, h, k).wait_send()

    pq_sib().wait_send()
    pq_z().wait_send()
    for i in range(3):
        pq_x(i).wait_send()
        pq_a(i).wait_recv()
    pk_ref[...] = pka[...]
    for i in range(3):
        pq_a(i).wait_send()


def score_kernel(fu_ref, fi_ref, pk_ref, fu_out, fi_out, s_out):
    fu_out[...] = fu_ref[...]
    fi_out[...] = fi_ref[...]
    s_out[...] = dot(pk_ref[...], fi_ref[...], 1, 1)


def scores_of(fu, fi, picked):
    width = 256
    whole = lambda shape: pl.BlockSpec(shape, lambda i: (0, 0))
    return pl.pallas_call(
        score_kernel,
        grid=(STRIPE // width,),
        out_shape=(jax.ShapeDtypeStruct(fu.shape, BF), jax.ShapeDtypeStruct(fi.shape, BF),
                   jax.ShapeDtypeStruct((QUERIES, STRIPE), F32)),
        in_specs=[whole((UROWS, EMB)), pl.BlockSpec((width, EMB), lambda i: (i, 0)), whole((QUERIES, EMB))],
        out_specs=(whole((UROWS, EMB)), pl.BlockSpec((width, EMB), lambda i: (i, 0)),
                   pl.BlockSpec((QUERIES, width), lambda i: (0, i))),
        name='scores',
    )(fu, fi, picked)


def propagate(mask_blk, user_shard, item_shard, queries):
    vm = pl.BlockSpec(memory_space=pltpu.VMEM)
    dma = pltpu.SemaphoreType.DMA
    qh, qq = QUERIES // 2, QUERIES // 4
    scratch = [
        pltpu.VMEM((2 * ROWS, COLS), BF),
        pltpu.VMEM((8, NCH, EMB, CH), F32),
        pltpu.VMEM((4, NCH, EMB, CH), F32),
        pltpu.VMEM((2, NCH, EMB, CH), F32),
        pltpu.VMEM((2, COLS, EMB), BF),
        pltpu.VMEM((LAYERS, EMB, 2 * ROWS), BF),
        pltpu.VMEM((2 * ROWS, EMB), F32),
        pltpu.VMEM((ROWS, EMB), F32),
        pltpu.VMEM((UROWS, EMB), F32),
        pltpu.VMEM((1, COLS), F32),
        pltpu.VMEM((NLOAD, LROWS, STRIPE), jnp.int32),
        pltpu.VMEM((NSTAGE, LROWS, STRIPE), BF),
        pltpu.VMEM((2, 8, STRIPE), F32),
        pltpu.VMEM((2, CHIPS, 8, STRIPE // 8), F32),
        pltpu.VMEM((7, CHIPS, 8, STRIPE // 8), F32),
        pltpu.VMEM((8, ROWS), F32),
        pltpu.VMEM((3, 8, ROWS), F32),
        pltpu.VMEM((UROWS, EMB), F32),
        pltpu.VMEM((QUERIES, EMB), BF),
        pltpu.VMEM((qh, EMB), BF),
        pltpu.VMEM((qq, EMB), BF),
        pltpu.VMEM((3, qq, EMB), BF),
        pltpu.VMEM((QUERIES, EMB), BF),
        dma((NLOAD,)), dma((NSTAGE,)), dma((CHIPS,)),
        dma((2, 4, NCH)), dma((2, 4, NCH)),
        dma((2, 2, NCH)), dma((2, 2, NCH)),
        dma((2, 2, 2, NCH)), dma((2, 2, 2, NCH)),
        dma((2, 2, NCH)), dma((2, 2, NCH)),
        dma((LAYERS,)), dma((LAYERS,)), dma((LAYERS,)), dma((LAYERS,)),
        dma((LAYERS, 3)), dma((LAYERS, 3)),
        dma((3,)), dma((3,)), dma((7, CHIPS)), dma((7, CHIPS)), dma((3,)), dma((3,)), dma((8,)), dma((8,)),
    ]
    return pl.pallas_call(
        kernel,
        out_shape=(jax.ShapeDtypeStruct((UROWS, EMB), BF),
                   jax.ShapeDtypeStruct((STRIPE, EMB), BF),
                   jax.ShapeDtypeStruct((QUERIES, EMB), BF)),
        in_specs=[pl.BlockSpec(memory_space=pl.ANY), vm, vm, vm],
        out_specs=(vm, vm, vm),
        scratch_shapes=scratch,
        compiler_params=pltpu.CompilerParams(collective_id=0, has_side_effects=True,
                                             vmem_limit_bytes=67043328),
        name='propagate',
    )(mask_blk, user_shard, item_shard, queries)


def solution(mesh):
    def device_step(mask_blk, user_shard, item_shard, queries):
        fu, fi, picked = propagate(mask_blk, user_shard, item_shard, queries.reshape(1, QUERIES))
        return scores_of(fu, fi, picked)

    return jax.shard_map(
        device_step, mesh=mesh,
        in_specs=(P('row', 'col'), P(('row', 'col'), None), P(('col', 'row'), None), P()),
        out_specs=(P(('row', 'col'), None), P(('col', 'row'), None), P(None, ('col', 'row'))),
        check_vma=False)
```

time: 197 us -> 195 us (0.990)
  matrix products: 5.84 us -> 0 us
  Pallas kernels: 189 us -> 194 us
    pallas_call x0 -> x1, Pallas kernels: none -> 7.06 us  [scores_of(): pl.pallas_call(score_kernel, grid=(STRIPE // width,), out_shape=(jax.Shap...]
    dot_general x1 -> x0, matrix products: 5.84 us -> none  [device_step(): lax.dot_general(picked, fi, (((1,), (1,)), ((), ())), preferred_element_t...]
    pallas_call x1, Pallas kernels: 189 us -> 186 us  [propagate(): pl.pallas_call(kernel, out_shape=(jax.ShapeDtypeStruct((UROWS, EMB), BF),...]
where the time goes in v2:
time: 195 us; the launch traced here: 194 us
  Pallas kernels  194 us (99%)
    pallas_call x1, Pallas kernels, propagate(): pl.pallas_call(kernel, out_shape=(jax.ShapeDtypeStruct((UROWS, EMB), BF),...  186 us
    pallas_call x1, Pallas kernels, scores_of(): pl.pallas_call(score_kernel, grid=(STRIPE // width,), out_shape=(jax.Shap...  7.06 us

profile of v2, /device:TPU:0, one launch (start us, length us, event | category | flops | bytes accessed | tf_op | source)
XLA Modules:
  0.0 194.1 jit_solution(14992457360766485814)
XLA Ops:
  0.6 186.4 %propagate.1 = (bf16[512,128]{1,0:T(8,128)(2,1)}, bf16[2048,128]{1,0:T(8,128)(2,1)}, bf16[1024,128]{1,0:T(8,128)(2,1)}) custom-call(s32[1024,16384]{1,0:T(8,128)} %mask_ref.1, bf16[512,128]{1,0:T(8,128)(2,1)} %ue_ref.1, bf16[2048,128]{1,0:T(8,128)(2,1)} %ie_ref.1, s32[1,1024]{1,0:T(1,128)} %bitcast.1), custom_call_target="tpu_custom_call" | custom-call | tf_op jit(solution)/shard_map/propagate/pallas_call | solution.py:542
  187.1 7.1 %scores.1 = (bf16[512,128]{1,0:T(8,128)(2,1)}, bf16[2048,128]{1,0:T(8,128)(2,1)}, f32[1024,2048]{1,0:T(8,128)}) custom-call(bf16[512,128]{1,0:T(8,128)(2,1)} %get-tuple-element.6.fu_ref, bf16[2048,128]{1,0:T(8,128)(2,1)} %get-tuple-element.7.fi_ref, bf16[1024,128]{1,0:T(8,128)(2,1)} %get-tuple-element.8.pk_ref), custom_call_target="tpu_custom_call" | custom-call | tf_op jit(solution)/shard_map/scores/pallas_call | solution.py:493

commit v3 on v2

--- a/solution.py
+++ b/solution.py
@@ -21,8 +21,10 @@
 CH = HALF // NCH
 LROWS = 128
 NLOAD = 6
-NSTAGE = 8
+NSTAGE = 11
+N_HELD = 8
 QUERIES = 1024
+SROWS = 128
 
 
 def al(v, m):
@@ -33,11 +35,11 @@
     return lax.dot_general(a, b, (((ca,), (cb,)), ((), ())), preferred_element_type=F32)
 
 
-def kernel(mask_ref, ue_ref, ie_ref, q_ref, fu_ref, fi_ref, pk_ref,
+def kernel(mask_ref, ue_hbm, ie_hbm, q_hbm, fu_hbm, fi_hbm, pk_hbm, ue_ref, ie_ref, q_ref, fu_ref, fi_ref, pkf,
            a, part, r1, r2, panel, eut, upart, ursib, urz, invi, mbuf, stage,
            cs, dcs, dcr, dus, dur, usum, pkc, pks, pkz, pkx, pka,
            lsem, xs, xr, s1s, s1r, s2s, s2r, ags, agr, fws, fwr,
-           usibs, usibr, uzs, uzr, uas, uar, eis, eir, dgs, dgr, dvs, dvr, pqs, pqr):
+           usibs, usibr, uzs, uzr, uas, uar, eis, eir, dgs, dgr, dvs, dvr, pqs, pqr, ins, outs, fis):
     row = lax.axis_index('row')
     z = lax.axis_index('col')
     c = lax.rem(row, 2)
@@ -85,16 +87,15 @@
         par = first * (1 - lax.div(w, n_group)) + (1 - first) * lax.rem(w, 2)
         return load_at(i, rg, par, n)
 
+    inputs = [pltpu.make_async_copy(src, dst, ins.at[i])
+              for i, (src, dst) in enumerate(((ie_hbm, ie_ref), (ue_hbm, ue_ref), (q_hbm, q_ref)))]
+    for cp in inputs:
+        cp.start()
     for n in range(NLOAD):
         load(jnp.int32(n)).start()
-
-    ucol = al(c * ROWS + z * UROWS, UROWS)
-    usum[...] = ue_ref[...].astype(F32)
-    eut[0, :, pl.ds(ucol, UROWS)] = ue_ref[...].astype(F32).T.astype(BF)
-    own_rows = pl.ds(al(me * STRIPE, STRIPE), STRIPE)
-    panel[0, own_rows, :] = ie_ref[...]
     cs[...] = jnp.zeros_like(cs)
     upart[pl.ds(0, ROWS), :] = jnp.zeros((ROWS, EMB), F32)
+    ucol = al(c * ROWS + z * UROWS, UROWS)
 
     def count(i, rg, par, n, sslot):
         p = stripe(i)
@@ -121,18 +122,20 @@
         def _():
             load(n + NLOAD).start()
 
-    def xcopy(i, rg):
-        slot = lax.rem(i * n_group + rg, NSTAGE)
+    def xcopy(m):
+        i = lax.div(m, n_group)
+        rg = lax.rem(m, n_group)
+        slot = lax.rem(m, NSTAGE)
         return rcopy(stage.at[slot],
                      a.at[pl.ds(al(c * ROWS + rg * LROWS, LROWS), LROWS), pl.ds(al(stripe(i) * STRIPE, STRIPE), STRIPE)],
                      xs.at[slot], xr.at[i], sib)
 
     def dgsend(p, i):
-        return rcopy(dcs.at[(1, 1, 1, 0, 0, 0, 0)[i], p], dcr.at[i, p], dgs.at[i, p], dgr.at[i, p],
+        return rcopy(dcs.at[(1, 1, 1, 0, 0, 0, 0)[i], p], dcr.at[i, p], dgs, dgr,
                      (xn, yn, dg, sib, xnc, ync, dgc)[i])
 
     def dusend(i):
-        return rcopy(dus, dur.at[i], dvs.at[i], dvr.at[i], (zn, sib, zsib)[i])
+        return rcopy(dus, dur.at[i], dvs, dvr, (zn, sib, zsib)[i])
 
     def stripe_degrees(i):
         p = stripe(i)
@@ -149,33 +152,60 @@
         return 0
 
     lax.fori_loop(0, n_group, own_first, 0)
+    for cp in inputs:
+        cp.wait()
+    usum[...] = ue_ref[...].astype(F32)
+    eut[0, :, pl.ds(ucol, UROWS)] = ue_ref[...].astype(F32).T.astype(BF)
+    own_rows = pl.ds(al(me * STRIPE, STRIPE), STRIPE)
+    panel[0, own_rows, :] = ie_ref[...]
     pl.semaphore_wait(barrier, len(peers))
 
+    def half_rows(q, h):
+        return pl.ds(al(q * STRIPE + h * HALF, HALF), HALF)
+
     def ei0(i):
-        return rcopy(ie_ref, panel.at[0, own_rows], eis.at[i], eir.at[i], (xn, yn, dg)[i])
+        q, h, to = ((me, 0, xn), (me, 1, yn), (me, 1, xn), (me, 0, yn), (y * 2 + ox, 0, yn), (oy * 2 + x, 1, xn))[i]
+        blk = panel.at[0, half_rows(q, h)]
+        src = ie_ref.at[pl.ds(h * HALF, HALF)] if i < 4 else blk
+        return rcopy(src, blk, eis, eir.at[min(i, 2)], to)
 
     def ua(j, i):
         blk = eut.at[j, :, pl.ds(ucol, UROWS)]
-        return rcopy(blk, blk, uas.at[j, i], uar.at[j, i], (zn, sib, zsib)[i])
-
-    def sib_first(rg, _):
-        count(0, rg, 0, n_group + rg, rg)
-        xcopy(0, rg).start()
-        return 0
-
-    lax.fori_loop(0, n_group, sib_first, 0)
-    for i in range(3):
+        return rcopy(blk, blk, uas.at[j], uar.at[j], (zn, sib, zsib)[i])
+
+    for i in range(4):
         ei0(i).start()
     for i in range(3):
         ua(0, i).start()
+
+    def sib_first(rg, _):
+        count(0, rg, 0, n_group + rg, rg)
+        xcopy(rg).start()
+        return 0
+
+    lax.fori_loop(0, n_group, sib_first, 0)
     stripe_degrees(0)
 
     def mask_step(m, _):
         i = lax.div(m, n_group)
         rg = lax.rem(m, n_group)
-        xcopy(i - 1, rg).wait_send()
-        count(i, rg, 0, 2 * m, rg)
-        xcopy(i, rg).start()
+        w = m - n_group
+
+        @pl.when(m >= NSTAGE)
+        def _():
+            xcopy(m - NSTAGE).wait_send()
+        count(i, rg, 0, 2 * m, lax.rem(m, NSTAGE))
+
+        @pl.when(lax.rem(w, 3) != 0)
+        def _():
+            xcopy(n_group + lax.div(2 * w, 3)).start()
+
+        @pl.when(m == 2 * n_group)
+        def _():
+            ei0(0).wait_recv()
+            ei0(4).start()
+            ei0(1).wait_recv()
+            ei0(5).start()
         count(i, rg, 1, 2 * m + 1, 0)
 
         @pl.when(i == CHIPS - 1)
@@ -193,26 +223,25 @@
 
     for i in range(3):
         dusend(i).start()
-
-    def stripe_inverse(i):
-        p = stripe(i)
-        for k in range(7):
-            dgsend(p, k).wait_recv()
+    for k in range(N_HELD):
+        xcopy(jnp.int32(CHIPS * n_group - N_HELD + k)).start()
+
+    def all_of(ref, ss, rs):
+        return rcopy(ref, ref, ss, rs, sib)
+
+    def swapped(i):
+        region = a.at[pl.ds(al(oc * ROWS, ROWS), ROWS), pl.ds(al(stripe(i) * STRIPE, STRIPE), STRIPE)]
+        rcopy(region, region, xs.at[0], xr.at[i], sib).wait_recv()
+
+    all_of(dcr, dgs, dgr).wait_recv()
+    for p in range(CHIPS):
         v = dcs[1, p]
         for k in range(7):
             v = v + dcr[k, p]
         v = lax.rsqrt(jnp.maximum(v, 1.0))
         for g in range(8):
-            invi[0:1, pl.ds(al(p * STRIPE + g * 256, 256), 256)] = v[g:g + 1, :]
-
-    def swapped(i):
-        region = a.at[pl.ds(al(oc * ROWS, ROWS), ROWS), pl.ds(al(stripe(i) * STRIPE, STRIPE), STRIPE)]
-        rcopy(region, region, xs.at[0], xr.at[i], sib).wait_recv()
-
-    for i in range(3):
-        stripe_inverse(i)
-    for i in range(3):
-        dusend(i).wait_recv()
+            invi[0:1, p * STRIPE + g * 256:p * STRIPE + (g + 1) * 256] = v[g:g + 1, :]
+    all_of(dur, dvs, dvr).wait_recv()
     for blk, v in ((c, dus[...] + dur[0]), (oc, dur[1] + dur[2])):
         v = lax.rsqrt(jnp.maximum(v, 1.0))
         for b in range(ROWS // 128):
@@ -232,22 +261,23 @@
     def s1(st, t, k):
         h = lax.rem(t, 2)
         to = dev(x + (1 - h) * (1 - 2 * x), y + h * (1 - 2 * y), c, z)
-        return rcopy(part.at[t, k], r1.at[t, k], s1s.at[st, t, k], s1r.at[st, t, k], to)
+        return rcopy(part.at[t, k], r1.at[t, k], s1s, s1r.at[st, k], to)
 
     def s2(st, h, k):
-        return rcopy(part.at[4 + h, k], r2.at[h, k], s2s.at[st, h, k], s2r.at[st, h, k], (yn, xn)[h])
+        return rcopy(part.at[4 + h, k], r2.at[h, k], s2s, s2r.at[st, k], (yn, xn)[h])
 
     def chunk_rows(q, h, k):
         return pl.ds(al(q * STRIPE + h * HALF + k * CH, CH), CH)
 
     def ag(st, d, h, k):
         blk = panel.at[1 - st, chunk_rows(me, h, k)]
-        return rcopy(blk, blk, ags.at[st, d, h, k], agr.at[st, d, h, k], (xn, yn)[d])
+        rs = agr.at[st, k] if d == h else agr.at[st, NCH]
+        return rcopy(blk, blk, ags.at[st], rs, (xn, yn)[d])
 
     def fw(st, h, k):
         q = (y * 2 + ox, oy * 2 + x)[h]
         blk = panel.at[1 - st, chunk_rows(q, h, k)]
-        return rcopy(blk, blk, fws.at[st, h, k], fwr.at[st, h, k], (yn, xn)[h])
+        return rcopy(blk, blk, fws.at[st], fwr.at[st], (yn, xn)[h])
 
     def usib(j):
         return rcopy(upart.at[pl.ds(al(oc * ROWS, ROWS), ROWS)], ursib, usibs.at[j], usibr.at[j], sib)
@@ -260,16 +290,18 @@
     quarter = pl.ds(al(c * qh + z * qq, qq), qq)
 
     def pq_sib():
-        return rcopy(pkc.at[pl.ds(al(oc * qh, qh), qh)], pks, pqs.at[0], pqr.at[0], sib)
+        return rcopy(pkc.at[pl.ds(al(oc * qh, qh), qh)], pks, pqs, pqr.at[0], sib)
 
     def pq_z():
-        return rcopy(pkc.at[pl.ds(al(c * qh + oz * qq, qq), qq)], pkz, pqs.at[1], pqr.at[1], zn)
+        return rcopy(pkc.at[pl.ds(al(c * qh + oz * qq, qq), qq)], pkz, pqs, pqr.at[1], zn)
 
     def pq_x(i):
-        return rcopy(pkc.at[quarter], pkx.at[i], pqs.at[2 + i], pqr.at[2 + i], (xn, yn, dg)[i])
+        h, to = ((0, xn), (1, yn), (0, yn), (1, xn))[i]
+        src = (pkc if i < 2 else pka).at[pl.ds(al(c * qh + z * qq + h * (qq // 2), qq // 2), qq // 2)]
+        return rcopy(src, pkx.at[i], pqs, pqr.at[2 + i // 2], to)
 
     def pq_a(i):
-        return rcopy(pka.at[quarter], pka.at[quarter], pqs.at[5 + i], pqr.at[5 + i], (zn, sib, zsib)[i])
+        return rcopy(pkf.at[quarter], pkf.at[quarter], pqs, pqr.at[4], (zn, sib, zsib)[i])
 
     def badd(u, v):
         return (u.astype(F32) + v.astype(F32)).astype(BF)
@@ -284,11 +316,20 @@
             return 0
         lax.fori_loop(0, 2 * ROWS // 128, norm, 0)
 
+    def fu_out():
+        return pltpu.make_async_copy(fu_ref, fu_hbm, outs.at[0])
+
+    def pk_out():
+        return pltpu.make_async_copy(pkf, pk_hbm, outs.at[1])
+
+    def fi_out(h, k):
+        loc = pl.ds(al(h * HALF + k * CH, CH), CH)
+        return pltpu.make_async_copy(fi_ref.at[loc], fi_hbm.at[loc], fis)
+
     for j in range(LAYERS):
         st = j % 2
         last = j == LAYERS - 1
-        for i in range(3):
-            ua(j, i).wait_recv()
+        all_of(eut.at[j, :, pl.ds(0, 3 * UROWS)], uas.at[j], uar.at[j]).wait_recv()
 
         def item_tile(t, _):
             base = al(tile_q(t) * STRIPE + lax.rem(t, 2) * HALF, HALF)
@@ -315,17 +356,16 @@
             return 0
 
         def stage1(k, _):
+            all_of(r1.at[:, k], s1s, s1r.at[st, k]).wait_recv()
             for h in range(2):
-                s1(st, 2 + h, k).wait_recv()
                 part[4 + h, k] = part[4 + h, k] + r1[2 + h, k]
-                s1(st, h, k).wait_recv()
                 part[6 + h, k] = part[6 + h, k] + r1[h, k]
                 s2(st, h, k).start()
             return 0
 
         def stage2(k, _):
+            all_of(r2.at[:, k], s2s, s2r.at[st, k]).wait_recv()
             for h in range(2):
-                s2(st, h, k).wait_recv()
                 e = (part[6 + h, k] + r2[h, k]).T.astype(BF)
                 rsl = chunk_rows(me, h, k)
                 if last:
@@ -333,6 +373,7 @@
                     tot = ie_ref[loc, :].astype(F32) + panel[1, rsl, :].astype(F32)
                     tot = tot + panel[0, rsl, :].astype(F32) + e.astype(F32)
                     fi_ref[loc, :] = (tot * (1.0 / (LAYERS + 1))).astype(BF)
+                    fi_out(h, k).start()
                 else:
                     panel[1 - st, rsl, :] = e
                     ag(st, 0, h, k).start()
@@ -340,9 +381,8 @@
             return 0
 
         def forward(k, _):
-            ag(st, 0, 0, k).wait_recv()
+            all_of(panel.at[1 - st, pl.ds(0, 2 * CH)], ags.at[st], agr.at[st, k]).wait_recv()
             fw(st, 0, k).start()
-            ag(st, 1, 1, k).wait_recv()
             fw(st, 1, k).start()
             return 0
 
@@ -369,18 +409,15 @@
 
         def users():
             if j == 0:
-                for i in range(3):
-                    ei0(i).wait_recv()
+                all_of(panel.at[0, pl.ds(0, 4 * HALF)], eis, eir.at[2]).wait_recv()
             else:
-                for k in range(NCH):
-                    ag(1 - st, 0, 1, k).wait_recv()
-                    ag(1 - st, 1, 0, k).wait_recv()
+                all_of(panel.at[st, pl.ds(0, STRIPE)], ags.at[1 - st], agr.at[1 - st, NCH]).wait_recv()
             lax.fori_loop(0, 4, user_near, 0)
             if j > 0:
-                for k in range(NCH):
-                    fw(1 - st, 0, k).wait_recv()
-                    fw(1 - st, 1, k).wait_recv()
+                all_of(panel.at[st, pl.ds(0, STRIPE)], fws.at[1 - st], fwr.at[1 - st]).wait_recv()
             lax.fori_loop(0, 4, user_far, 0)
+
+        def users_out():
             usib(j).wait_recv()
             mine = pl.ds(al(c * ROWS, ROWS), ROWS)
             upart[mine, :] = upart[mine, :] + ursib[...]
@@ -397,6 +434,7 @@
                 return
             fu = (usum[...] * (1.0 / (LAYERS + 1))).astype(BF)
             fu_ref[...] = fu
+            fu_out().start()
             ids = lax.broadcasted_iota(jnp.int32, (UROWS, QUERIES), 0) + (row * 2 + z) * UROWS
             hot = jnp.where(ids == q_ref[...], 1.0, 0.0).astype(BF)
             pkc[...] = dot(hot, fu, 0, 0).astype(BF)
@@ -407,106 +445,119 @@
             lax.fori_loop(2, 4, send_tile, 0)
             lax.fori_loop(4, 6, item_tile, 0)
             swapped(3)
-            stripe_inverse(3)
             lax.fori_loop(6, 8, item_tile, 0)
             lax.fori_loop(0, NCH - 1, stage1, 0)
             users()
+            users_out()
             stage1(NCH - 1, 0)
             lax.fori_loop(0, NCH, stage2, 0)
             user_final()
         else:
-            lax.fori_loop(0, 4, send_tile, 0)
+            lax.fori_loop(0, 2, send_tile, 0)
             users()
+            users_out()
+            lax.fori_loop(2, 4, send_tile, 0)
             lax.fori_loop(4, 8, item_tile, 0)
-            lax.fori_loop(0, 2, stage1, 0)
+            if not last:
+                lax.fori_loop(0, 2, stage1, 0)
             user_final()
             if last:
                 pq_sib().wait_recv()
                 hrows = pl.ds(al(c * qh, qh), qh)
                 pkc[hrows, :] = badd(pkc[hrows, :], pks[...])
                 pq_z().start()
+                stage1(0, 0)
                 pq_z().wait_recv()
                 pkc[quarter, :] = badd(pkc[quarter, :], pkz[...])
-                for i in range(3):
+                for i in range(2):
+                    pq_x(i).start()
+                stage1(1, 0)
+                all_of(pkx.at[pl.ds(0, 2)], pqs, pqr.at[2]).wait_recv()
+                for i in range(2):
+                    rsl = pl.ds(al(c * qh + z * qq + i * (qq // 2), qq // 2), qq // 2)
+                    pka[rsl, :] = badd(pkc[rsl, :], pkx[i])
+                for i in range(2, 4):
                     pq_x(i).start()
             lax.fori_loop(2, NCH, stage1, 0)
-            lax.fori_loop(0, NCH - 1, stage2, 0)
+            lax.fori_loop(0, 2, stage2, 0)
             if last:
-                for i in range(3):
-                    pq_x(i).wait_recv()
-                pka[quarter, :] = badd(badd(pkc[quarter, :], pkx[0]), badd(pkx[1], pkx[2]))
+                all_of(pkx.at[pl.ds(2, 2)], pqs, pqr.at[3]).wait_recv()
+                for i in range(2, 4):
+                    rsl = pl.ds(al(c * qh + z * qq + (i - 2) * (qq // 2), qq // 2), qq // 2)
+                    pkf[rsl, :] = badd(pka[rsl, :], pkx[i])
                 for i in range(3):
                     pq_a(i).start()
-            stage2(NCH - 1, 0)
+            lax.fori_loop(2, NCH, stage2, 0)
         if not last:
             lax.fori_loop(0, NCH, forward, 0)
 
         usib(j).wait_send()
         uz(j).wait_send()
-        for i in range(3):
-            ua(j, i).wait_send()
-        for k in range(NCH):
-            for t in range(4):
-                s1(st, t, k).wait_send()
-            for h in range(2):
-                s2(st, h, k).wait_send()
+        all_of(eut.at[j, :, pl.ds(0, 3 * UROWS)], uas.at[j], uar.at[j]).wait_send()
+        all_of(part.at[pl.ds(0, 4)], s1s, s1r.at[st, 0]).wait_send()
+        all_of(part.at[pl.ds(4, 2)], s2s, s2r.at[st, 0]).wait_send()
         if j == 0:
-            def drain_degrees(p, _):
-                for k in range(7):
-                    dgsend(p, k).wait_send()
+            all_of(dcr, dgs, dgr).wait_send()
+            all_of(dur, dvs, dvr).wait_send()
+            def drain_swap(m, _):
+                xcopy(m).wait_send()
                 return 0
-            lax.fori_loop(0, CHIPS, drain_degrees, 0)
-
-            def drain_swap(rg, _):
-                xcopy(CHIPS - 1, rg).wait_send()
-                return 0
-            lax.fori_loop(0, n_group, drain_swap, 0)
-            for i in range(3):
-                dusend(i).wait_send()
-                ei0(i).wait_send()
+            lax.fori_loop(CHIPS * n_group - NSTAGE, CHIPS * n_group, drain_swap, 0)
+            all_of(panel.at[0, pl.ds(0, 6 * HALF)], eis, eir.at[2]).wait_send()
         else:
-            for k in range(NCH):
-                for h in range(2):
-                    ag(1 - st, 0, h, k).wait_send()
-                    ag(1 - st, 1, h, k).wait_send()
-                    fw(1 - st, h, k).wait_send()
-
-    pq_sib().wait_send()
-    pq_z().wait_send()
-    for i in range(3):
-        pq_x(i).wait_send()
-        pq_a(i).wait_recv()
-    pk_ref[...] = pka[...]
-    for i in range(3):
-        pq_a(i).wait_send()
-
-
-def score_kernel(fu_ref, fi_ref, pk_ref, fu_out, fi_out, s_out):
-    fu_out[...] = fu_ref[...]
-    fi_out[...] = fi_ref[...]
-    s_out[...] = dot(pk_ref[...], fi_ref[...], 1, 1)
+            all_of(panel.at[st, pl.ds(0, 2 * STRIPE)], ags.at[1 - st], agr.at[1 - st, NCH]).wait_send()
+            all_of(panel.at[st, pl.ds(0, STRIPE)], fws.at[1 - st], fwr.at[1 - st]).wait_send()
+
+    all_of(pkf.at[pl.ds(0, 3 * qq)], pqs, pqr.at[4]).wait_recv()
+    pk_out().start()
+    all_of(fi_ref, pqs, pqr.at[4]).wait_send()
+    pltpu.make_async_copy(fi_ref, fi_hbm, fis).wait()
+    fu_out().wait()
+    pk_out().wait()
+
+
+def score_kernel(fu_ref, fi_ref, pk_ref, fu_out, fi_out, s_out, buf, sem, out_sem):
+    copies = [pltpu.make_async_copy(fu_ref, fu_out, out_sem.at[0]),
+              pltpu.make_async_copy(fi_ref, fi_out, out_sem.at[1])]
+    for i in range(QUERIES // SROWS):
+        rsl = pl.ds(i * SROWS, SROWS)
+        buf[i] = dot(pk_ref[rsl, :], fi_ref[...], 1, 1)
+        copies.append(pltpu.make_async_copy(buf.at[i], s_out.at[rsl, :], sem.at[i]))
+        if i == 0:
+            for cp in copies:
+                cp.start()
+        else:
+            copies[-1].start()
+    for cp in copies:
+        cp.wait()
 
 
 def scores_of(fu, fi, picked):
-    width = 256
-    whole = lambda shape: pl.BlockSpec(shape, lambda i: (0, 0))
+    vm = pl.BlockSpec(memory_space=pltpu.VMEM)
+    hbm = pl.BlockSpec(memory_space=pl.ANY)
     return pl.pallas_call(
         score_kernel,
-        grid=(STRIPE // width,),
         out_shape=(jax.ShapeDtypeStruct(fu.shape, BF), jax.ShapeDtypeStruct(fi.shape, BF),
                    jax.ShapeDtypeStruct((QUERIES, STRIPE), F32)),
-        in_specs=[whole((UROWS, EMB)), pl.BlockSpec((width, EMB), lambda i: (i, 0)), whole((QUERIES, EMB))],
-        out_specs=(whole((UROWS, EMB)), pl.BlockSpec((width, EMB), lambda i: (i, 0)),
-                   pl.BlockSpec((QUERIES, width), lambda i: (0, i))),
+        in_specs=[vm, vm, vm],
+        out_specs=(hbm, hbm, hbm),
+        scratch_shapes=[pltpu.VMEM((QUERIES // SROWS, SROWS, STRIPE), F32),
+                        pltpu.SemaphoreType.DMA((QUERIES // SROWS,)), pltpu.SemaphoreType.DMA((2,))],
         name='scores',
     )(fu, fi, picked)
 
 
 def propagate(mask_blk, user_shard, item_shard, queries):
-    vm = pl.BlockSpec(memory_space=pltpu.VMEM)
+    hbm = pl.BlockSpec(memory_space=pl.ANY)
     dma = pltpu.SemaphoreType.DMA
     qh, qq = QUERIES // 2, QUERIES // 4
     scratch = [
+        pltpu.VMEM((UROWS, EMB), BF),
+        pltpu.VMEM((STRIPE, EMB), BF),
+        pltpu.VMEM((1, QUERIES), jnp.int32),
+        pltpu.VMEM((UROWS, EMB), BF),
+        pltpu.VMEM((STRIPE, EMB), BF),
+        pltpu.VMEM((QUERIES, EMB), BF),
         pltpu.VMEM((2 * ROWS, COLS), BF),
         pltpu.VMEM((8, NCH, EMB, CH), F32),
         pltpu.VMEM((4, NCH, EMB, CH), F32),
@@ -528,24 +579,26 @@
         pltpu.VMEM((QUERIES, EMB), BF),
         pltpu.VMEM((qh, EMB), BF),
         pltpu.VMEM((qq, EMB), BF),
-        pltpu.VMEM((3, qq, EMB), BF),
+        pltpu.VMEM((4, qq // 2, EMB), BF),
         pltpu.VMEM((QUERIES, EMB), BF),
         dma((NLOAD,)), dma((NSTAGE,)), dma((CHIPS,)),
-        dma((2, 4, NCH)), dma((2, 4, NCH)),
-        dma((2, 2, NCH)), dma((2, 2, NCH)),
-        dma((2, 2, 2, NCH)), dma((2, 2, 2, NCH)),
-        dma((2, 2, NCH)), dma((2, 2, NCH)),
+        dma, dma((2, NCH)),
+        dma, dma((2, NCH)),
+        dma((2,)), dma((2, NCH + 1)),
+        dma((2,)), dma((2,)),
         dma((LAYERS,)), dma((LAYERS,)), dma((LAYERS,)), dma((LAYERS,)),
-        dma((LAYERS, 3)), dma((LAYERS, 3)),
-        dma((3,)), dma((3,)), dma((7, CHIPS)), dma((7, CHIPS)), dma((3,)), dma((3,)), dma((8,)), dma((8,)),
+        dma((LAYERS,)), dma((LAYERS,)),
+        dma, dma((3,)), dma, dma, dma, dma,
+        dma, dma((5,)),
+        dma((3,)), dma((2,)), dma,
     ]
     return pl.pallas_call(
         kernel,
         out_shape=(jax.ShapeDtypeStruct((UROWS, EMB), BF),
                    jax.ShapeDtypeStruct((STRIPE, EMB), BF),
                    jax.ShapeDtypeStruct((QUERIES, EMB), BF)),
-        in_specs=[pl.BlockSpec(memory_space=pl.ANY), vm, vm, vm],
-        out_specs=(vm, vm, vm),
+        in_specs=[hbm] * 4,
+        out_specs=(hbm, hbm, hbm),
         scratch_shapes=scratch,
         compiler_params=pltpu.CompilerParams(collective_id=0, has_side_effects=True,
                                              vmem_limit_bytes=67043328),

time: 195 us -> 178 us (0.913)
  Pallas kernels: 194 us -> 177 us
    pallas_call x1, Pallas kernels: 186 us -> 172 us  [propagate(): pl.pallas_call(kernel, out_shape=(jax.ShapeDtypeStruct((UROWS, EMB), BF),...]
    pallas_call x1, Pallas kernels: 7.06 us -> 4.83 us  [scores_of(): pl.pallas_call(score_kernel, out_shape=(jax.ShapeDtypeStruct(fu.shape, BF...]
where the time goes in v3:
time: 178 us
  Pallas kernels  177 us (99%)
    pallas_call x1, Pallas kernels, propagate(): pl.pallas_call(kernel, out_shape=(jax.ShapeDtypeStruct((UROWS, EMB), BF),...  172 us
    pallas_call x1, Pallas kernels, scores_of(): pl.pallas_call(score_kernel, out_shape=(jax.ShapeDtypeStruct(fu.shape, BF...  4.83 us

profile of v3, /device:TPU:0, one launch (start us, length us, event | category | flops | bytes accessed | tf_op | source)
XLA Modules:
  0.0 178.0 jit_solution(15135356738090665309)
XLA Ops:
  0.6 172.4 %propagate.1 = (bf16[512,128]{1,0:T(8,128)(2,1)}, bf16[2048,128]{1,0:T(8,128)(2,1)}, bf16[1024,128]{1,0:T(8,128)(2,1)}) custom-call(s32[1024,16384]{1,0:T(8,128)} %mask_ref.1, bf16[512,128]{1,0:T(8,128)(2,1)} %ue_hbm.1, bf16[2048,128]{1,0:T(8,128)(2,1)} %ie_hbm.1, s32[1,1024]{1,0:T(1,128)} %bitcast.1), custom_call_target="tpu_custom_call" | custom-call | tf_op jit(solution)/shard_map/propagate/pallas_call | solution.py:595
  173.0 4.8 %scores.1 = (bf16[512,128]{1,0:T(8,128)(2,1)}, bf16[2048,128]{1,0:T(8,128)(2,1)}, f32[1024,2048]{1,0:T(8,128)}) custom-call(bf16[512,128]{1,0:T(8,128)(2,1)} %get-tuple-element.6.fu_ref, bf16[2048,128]{1,0:T(8,128)(2,1)} %get-tuple-element.7.fi_ref, bf16[1024,128]{1,0:T(8,128)(2,1)} %get-tuple-element.8.pk_ref), custom_call_target="tpu_custom_call" | custom-call | tf_op jit(solution)/shard_map/scores/pallas_call | solution.py:538

commit v4 on v3

--- a/solution.py
+++ b/solution.py
@@ -171,7 +171,7 @@
 
     def ua(j, i):
         blk = eut.at[j, :, pl.ds(ucol, UROWS)]
-        return rcopy(blk, blk, uas.at[j], uar.at[j], (zn, sib, zsib)[i])
+        return rcopy(blk, blk, uas, uar.at[j], (zn, sib, zsib)[i])
 
     for i in range(4):
         ei0(i).start()
@@ -233,6 +233,12 @@
         region = a.at[pl.ds(al(oc * ROWS, ROWS), ROWS), pl.ds(al(stripe(i) * STRIPE, STRIPE), STRIPE)]
         rcopy(region, region, xs.at[0], xr.at[i], sib).wait_recv()
 
+    all_of(dur, dvs, dvr).wait_recv()
+    for blk, v in ((c, dus[...] + dur[0]), (oc, dur[1] + dur[2])):
+        v = lax.rsqrt(jnp.maximum(v, 1.0))
+        for b in range(ROWS // 128):
+            w = jnp.broadcast_to(v[0:1, b * 128:(b + 1) * 128], (128, 128))
+            upart[pl.ds(al(blk * ROWS + b * 128, 128), 128), :] = w.T
     all_of(dcr, dgs, dgr).wait_recv()
     for p in range(CHIPS):
         v = dcs[1, p]
@@ -241,12 +247,6 @@
         v = lax.rsqrt(jnp.maximum(v, 1.0))
         for g in range(8):
             invi[0:1, p * STRIPE + g * 256:p * STRIPE + (g + 1) * 256] = v[g:g + 1, :]
-    all_of(dur, dvs, dvr).wait_recv()
-    for blk, v in ((c, dus[...] + dur[0]), (oc, dur[1] + dur[2])):
-        v = lax.rsqrt(jnp.maximum(v, 1.0))
-        for b in range(ROWS // 128):
-            w = jnp.broadcast_to(v[0:1, b * 128:(b + 1) * 128], (128, 128))
-            upart[pl.ds(al(blk * ROWS + b * 128, 128), 128), :] = w.T
     for i in range(3):
         swapped(i)
 
@@ -258,33 +258,33 @@
         fy = (1 - h) * f2 + h * f1
         return (y + fy - 2 * y * fy) * 2 + (x + fx - 2 * x * fx)
 
-    def s1(st, t, k):
+    def s1(st, t, k, cols=pl.ds(0, CH)):
         h = lax.rem(t, 2)
         to = dev(x + (1 - h) * (1 - 2 * x), y + h * (1 - 2 * y), c, z)
-        return rcopy(part.at[t, k], r1.at[t, k], s1s, s1r.at[st, k], to)
+        return rcopy(part.at[t, k, :, cols], r1.at[t, k, :, cols], s1s, s1r.at[k], to)
 
     def s2(st, h, k):
-        return rcopy(part.at[4 + h, k], r2.at[h, k], s2s, s2r.at[st, k], (yn, xn)[h])
+        return rcopy(part.at[4 + h, k], r2.at[h, k], s2s, s2r.at[k], (yn, xn)[h])
 
     def chunk_rows(q, h, k):
         return pl.ds(al(q * STRIPE + h * HALF + k * CH, CH), CH)
 
     def ag(st, d, h, k):
         blk = panel.at[1 - st, chunk_rows(me, h, k)]
-        rs = agr.at[st, k] if d == h else agr.at[st, NCH]
+        rs = agr.at[k] if d == h else agr.at[NCH]
         return rcopy(blk, blk, ags.at[st], rs, (xn, yn)[d])
 
     def fw(st, h, k):
         q = (y * 2 + ox, oy * 2 + x)[h]
         blk = panel.at[1 - st, chunk_rows(q, h, k)]
-        return rcopy(blk, blk, fws.at[st], fwr.at[st], (yn, xn)[h])
+        return rcopy(blk, blk, fws.at[st], fwr, (yn, xn)[h])
 
     def usib(j):
-        return rcopy(upart.at[pl.ds(al(oc * ROWS, ROWS), ROWS)], ursib, usibs.at[j], usibr.at[j], sib)
+        return rcopy(upart.at[pl.ds(al(oc * ROWS, ROWS), ROWS)], ursib, usibs, usibr, sib)
 
     def uz(j):
         return rcopy(upart.at[pl.ds(al(c * ROWS + oz * UROWS, UROWS), UROWS)], urz,
-                     uzs.at[j], uzr.at[j], zn)
+                     uzs, uzr, zn)
 
     qh, qq = QUERIES // 2, QUERIES // 4
     quarter = pl.ds(al(c * qh + z * qq, qq), qq)
@@ -329,7 +329,7 @@
     for j in range(LAYERS):
         st = j % 2
         last = j == LAYERS - 1
-        all_of(eut.at[j, :, pl.ds(0, 3 * UROWS)], uas.at[j], uar.at[j]).wait_recv()
+        all_of(eut.at[j, :, pl.ds(0, 3 * UROWS)], uas, uar.at[j]).wait_recv()
 
         def item_tile(t, _):
             base = al(tile_q(t) * STRIPE + lax.rem(t, 2) * HALF, HALF)
@@ -355,8 +355,17 @@
             s1(st, t, k).start()
             return 0
 
+        def first_half(n, _):
+            t = lax.rem(n, 2)
+            cols = pl.ds(al(lax.div(n, 2) * 128, 128), 128)
+            base = al(tile_q(t) * STRIPE + t * HALF + lax.div(n, 2) * 128, 128)
+            normalise(base, 128)
+            part[t, 0, :, cols] = dot(eut[j], a[:, pl.ds(base, 128)], 1, 0)
+            s1(st, t, 0, cols).start()
+            return 0
+
         def stage1(k, _):
-            all_of(r1.at[:, k], s1s, s1r.at[st, k]).wait_recv()
+            all_of(r1.at[:, k], s1s, s1r.at[k]).wait_recv()
             for h in range(2):
                 part[4 + h, k] = part[4 + h, k] + r1[2 + h, k]
                 part[6 + h, k] = part[6 + h, k] + r1[h, k]
@@ -364,7 +373,7 @@
             return 0
 
         def stage2(k, _):
-            all_of(r2.at[:, k], s2s, s2r.at[st, k]).wait_recv()
+            all_of(r2.at[:, k], s2s, s2r.at[k]).wait_recv()
             for h in range(2):
                 e = (part[6 + h, k] + r2[h, k]).T.astype(BF)
                 rsl = chunk_rows(me, h, k)
@@ -381,7 +390,7 @@
             return 0
 
         def forward(k, _):
-            all_of(panel.at[1 - st, pl.ds(0, 2 * CH)], ags.at[st], agr.at[st, k]).wait_recv()
+            all_of(panel.at[1 - st, pl.ds(0, 2 * CH)], ags.at[st], agr.at[k]).wait_recv()
             fw(st, 0, k).start()
             fw(st, 1, k).start()
             return 0
@@ -394,6 +403,10 @@
                 d = dot(a[rsl, ks], panel[st, ks, :], 1, 0)
                 tot = d if tot is None else tot + d
             upart[rsl, :] = tot
+            if j == 0:
+                @pl.when(i == 2)
+                def _():
+                    stage1(2, 0)
             return 0
 
         def user_far(i, _):
@@ -411,10 +424,13 @@
             if j == 0:
                 all_of(panel.at[0, pl.ds(0, 4 * HALF)], eis, eir.at[2]).wait_recv()
             else:
-                all_of(panel.at[st, pl.ds(0, STRIPE)], ags.at[1 - st], agr.at[1 - st, NCH]).wait_recv()
+                all_of(panel.at[st, pl.ds(0, STRIPE)], ags.at[1 - st], agr.at[NCH]).wait_recv()
             lax.fori_loop(0, 4, user_near, 0)
+            if j == 0:
+                stage1(3, 0)
+                stage2(0, 0)
             if j > 0:
-                all_of(panel.at[st, pl.ds(0, STRIPE)], fws.at[1 - st], fwr.at[1 - st]).wait_recv()
+                all_of(panel.at[st, pl.ds(0, STRIPE)], fws.at[1 - st], fwr).wait_recv()
             lax.fori_loop(0, 4, user_far, 0)
 
         def users_out():
@@ -441,16 +457,16 @@
             pq_sib().start()
 
         if j == 0:
-            lax.fori_loop(0, 2 * NCH, first_chunk, 0)
+            lax.fori_loop(0, 4, first_half, 0)
+            lax.fori_loop(2, 2 * NCH, first_chunk, 0)
             lax.fori_loop(2, 4, send_tile, 0)
             lax.fori_loop(4, 6, item_tile, 0)
             swapped(3)
             lax.fori_loop(6, 8, item_tile, 0)
-            lax.fori_loop(0, NCH - 1, stage1, 0)
+            lax.fori_loop(0, 2, stage1, 0)
             users()
             users_out()
-            stage1(NCH - 1, 0)
-            lax.fori_loop(0, NCH, stage2, 0)
+            lax.fori_loop(1, NCH, stage2, 0)
             user_final()
         else:
             lax.fori_loop(0, 2, send_tile, 0)
@@ -493,9 +509,9 @@
 
         usib(j).wait_send()
         uz(j).wait_send()
-        all_of(eut.at[j, :, pl.ds(0, 3 * UROWS)], uas.at[j], uar.at[j]).wait_send()
-        all_of(part.at[pl.ds(0, 4)], s1s, s1r.at[st, 0]).wait_send()
-        all_of(part.at[pl.ds(4, 2)], s2s, s2r.at[st, 0]).wait_send()
+        all_of(eut.at[j, :, pl.ds(0, 3 * UROWS)], uas, uar.at[j]).wait_send()
+        all_of(part.at[pl.ds(0, 4)], s1s, s1r.at[0]).wait_send()
+        all_of(part.at[pl.ds(4, 2)], s2s, s2r.at[0]).wait_send()
         if j == 0:
             all_of(dcr, dgs, dgr).wait_send()
             all_of(dur, dvs, dvr).wait_send()
@@ -505,8 +521,8 @@
             lax.fori_loop(CHIPS * n_group - NSTAGE, CHIPS * n_group, drain_swap, 0)
             all_of(panel.at[0, pl.ds(0, 6 * HALF)], eis, eir.at[2]).wait_send()
         else:
-            all_of(panel.at[st, pl.ds(0, 2 * STRIPE)], ags.at[1 - st], agr.at[1 - st, NCH]).wait_send()
-            all_of(panel.at[st, pl.ds(0, STRIPE)], fws.at[1 - st], fwr.at[1 - st]).wait_send()
+            all_of(panel.at[st, pl.ds(0, 2 * STRIPE)], ags.at[1 - st], agr.at[NCH]).wait_send()
+            all_of(panel.at[st, pl.ds(0, STRIPE)], fws.at[1 - st], fwr).wait_send()
 
     all_of(pkf.at[pl.ds(0, 3 * qq)], pqs, pqr.at[4]).wait_recv()
     pk_out().start()
@@ -582,12 +598,12 @@
         pltpu.VMEM((4, qq // 2, EMB), BF),
         pltpu.VMEM((QUERIES, EMB), BF),
         dma((NLOAD,)), dma((NSTAGE,)), dma((CHIPS,)),
-        dma, dma((2, NCH)),
-        dma, dma((2, NCH)),
-        dma((2,)), dma((2, NCH + 1)),
-        dma((2,)), dma((2,)),
-        dma((LAYERS,)), dma((LAYERS,)), dma((LAYERS,)), dma((LAYERS,)),
-        dma((LAYERS,)), dma((LAYERS,)),
+        dma, dma((NCH,)),
+        dma, dma((NCH,)),
+        dma((2,)), dma((NCH + 1,)),
+        dma((2,)), dma,
+        dma, dma, dma, dma,
+        dma, dma((LAYERS,)),
         dma, dma((3,)), dma, dma, dma, dma,
         dma, dma((5,)),
         dma((3,)), dma((2,)), dma,

time: 178 us -> 175 us (0.983)
  Pallas kernels: 177 us -> 174 us
    pallas_call x1, Pallas kernels: 172 us -> 170 us  [propagate(): pl.pallas_call(kernel, out_shape=(jax.ShapeDtypeStruct((UROWS, EMB), BF),...]
where the time goes in v4:
time: 175 us
  Pallas kernels  174 us (99%)
    pallas_call x1, Pallas kernels, propagate(): pl.pallas_call(kernel, out_shape=(jax.ShapeDtypeStruct((UROWS, EMB), BF),...  170 us
    pallas_call x1, Pallas kernels, scores_of(): pl.pallas_call(score_kernel, out_shape=(jax.ShapeDtypeStruct(fu.shape, BF...  4.83 us

profile of v4, /device:TPU:0, one launch (start us, length us, event | category | flops | bytes accessed | tf_op | source)
XLA Modules:
  0.0 175.2 jit_solution(59561455118721653)
XLA Ops:
  0.6 169.5 %propagate.1 = (bf16[512,128]{1,0:T(8,128)(2,1)}, bf16[2048,128]{1,0:T(8,128)(2,1)}, bf16[1024,128]{1,0:T(8,128)(2,1)}) custom-call(s32[1024,16384]{1,0:T(8,128)} %mask_ref.1, bf16[512,128]{1,0:T(8,128)(2,1)} %ue_hbm.1, bf16[2048,128]{1,0:T(8,128)(2,1)} %ie_hbm.1, s32[1,1024]{1,0:T(1,128)} %bitcast.1), custom_call_target="tpu_custom_call" | custom-call | tf_op jit(solution)/shard_map/propagate/pallas_call | solution.py:611
  170.2 4.8 %scores.1 = (bf16[512,128]{1,0:T(8,128)(2,1)}, bf16[2048,128]{1,0:T(8,128)(2,1)}, f32[1024,2048]{1,0:T(8,128)}) custom-call(bf16[512,128]{1,0:T(8,128)(2,1)} %get-tuple-element.6.fu_ref, bf16[2048,128]{1,0:T(8,128)(2,1)} %get-tuple-element.7.fi_ref, bf16[1024,128]{1,0:T(8,128)(2,1)} %get-tuple-element.8.pk_ref), custom_call_target="tpu_custom_call" | custom-call | tf_op jit(solution)/shard_map/scores/pallas_call | solution.py:554

commit v5 on v4

--- a/solution.py
+++ b/solution.py
@@ -67,13 +67,8 @@
     n_group = ROWS // LROWS
     n_load = n_group * 2 * CHIPS
 
-    def stripe(i):
-        fx = 1 - lax.rem(i, 2)
-        fy = lax.rem(lax.div(i + 1, 2), 2)
-        return (y + fy - 2 * y * fy) * 2 + (x + fx - 2 * x * fx)
-
     def load_at(i, rg, par, n):
-        s = 2 * stripe(i) + par * c + (1 - par) * oc
+        s = 2 * i + par * c + (1 - par) * oc
         slot = lax.rem(n, NLOAD)
         return pltpu.make_async_copy(
             mask_ref.at[pl.ds(al(rg * LROWS, LROWS), LROWS), pl.ds(al(s * STRIPE, STRIPE), STRIPE)],
@@ -98,10 +93,9 @@
     ucol = al(c * ROWS + z * UROWS, UROWS)
 
     def count(i, rg, par, n, sslot):
-        p = stripe(i)
         slot = lax.rem(n, NLOAD)
         load_at(i, rg, par, n).wait()
-        cols = pl.ds(al(p * STRIPE, STRIPE), STRIPE)
+        cols = pl.ds(al(i * STRIPE, STRIPE), STRIPE)
         acc = jnp.zeros((8, STRIPE), F32)
         for g in range(LROWS // 16):
             v = mbuf[slot, g * 16:(g + 1) * 16, :].astype(F32)
@@ -127,31 +121,28 @@
         rg = lax.rem(m, n_group)
         slot = lax.rem(m, NSTAGE)
         return rcopy(stage.at[slot],
-                     a.at[pl.ds(al(c * ROWS + rg * LROWS, LROWS), LROWS), pl.ds(al(stripe(i) * STRIPE, STRIPE), STRIPE)],
+                     a.at[pl.ds(al(c * ROWS + rg * LROWS, LROWS), LROWS), pl.ds(al(i * STRIPE, STRIPE), STRIPE)],
                      xs.at[slot], xr.at[i], sib)
 
     def dgsend(p, i):
-        return rcopy(dcs.at[(1, 1, 1, 0, 0, 0, 0)[i], p], dcr.at[i, p], dgs, dgr,
+        return rcopy(dcs.at[(1, 1, 1, 0, 0, 0, 0)[i], p], dcr.at[i, p], dgs, dgr.at[p // (CHIPS - 1) if isinstance(p, int) else lax.div(p, CHIPS - 1)],
                      (xn, yn, dg, sib, xnc, ync, dgc)[i])
 
     def dusend(i):
         return rcopy(dus, dur.at[i], dvs, dvr, (zn, sib, zsib)[i])
 
-    def stripe_degrees(i):
-        p = stripe(i)
-        for par in range(2):
-            v = jnp.sum(cs[par], axis=0, keepdims=True)
-            for g in range(8):
-                dcs[par, p, g:g + 1, :] = v[:, g * 256:(g + 1) * 256]
-        cs[...] = jnp.zeros_like(cs)
-        for k in range(7):
+    def stripe_degrees(p, par):
+        v = jnp.sum(cs[par], axis=0, keepdims=True)
+        for g in range(8):
+            dcs[par, p, g:g + 1, :] = v[:, g * 256:(g + 1) * 256]
+        cs[par] = jnp.zeros((8, STRIPE), F32)
+        for k in ((6, 5, 4, 3), (2, 1, 0))[par]:
             dgsend(p, k).start()
 
     def own_first(rg, _):
         count(0, rg, 1, rg, 0)
         return 0
 
-    lax.fori_loop(0, n_group, own_first, 0)
     for cp in inputs:
         cp.wait()
     usum[...] = ue_ref[...].astype(F32)
@@ -178,13 +169,16 @@
     for i in range(3):
         ua(0, i).start()
 
+    lax.fori_loop(0, n_group, own_first, 0)
+
     def sib_first(rg, _):
         count(0, rg, 0, n_group + rg, rg)
         xcopy(rg).start()
         return 0
 
     lax.fori_loop(0, n_group, sib_first, 0)
-    stripe_degrees(0)
+    for par in range(2):
+        stripe_degrees(0, par)
 
     def mask_step(m, _):
         i = lax.div(m, n_group)
@@ -206,23 +200,28 @@
             ei0(4).start()
             ei0(1).wait_recv()
             ei0(5).start()
+        @pl.when(rg == n_group - 1)
+        def _():
+            stripe_degrees(i, 0)
         count(i, rg, 1, 2 * m + 1, 0)
 
         @pl.when(i == CHIPS - 1)
         def _():
             rsl = pl.ds(al(rg * LROWS, LROWS), LROWS)
-            v = jnp.sum(upart[rsl, :].T, axis=0, keepdims=True)
-            dus[:, rsl] = jnp.broadcast_to(v, (8, LROWS))
+            dus[pl.ds(rg, 1), :] = jnp.sum(upart[rsl, :].T, axis=0, keepdims=True)
+
+        @pl.when(m == CHIPS * n_group - 1)
+        def _():
+            for k in range(3):
+                dusend(k).start()
 
         @pl.when(rg == n_group - 1)
         def _():
-            stripe_degrees(i)
+            stripe_degrees(i, 1)
         return 0
 
     lax.fori_loop(n_group, CHIPS * n_group, mask_step, 0)
 
-    for i in range(3):
-        dusend(i).start()
     for k in range(N_HELD):
         xcopy(jnp.int32(CHIPS * n_group - N_HELD + k)).start()
 
@@ -230,23 +229,26 @@
         return rcopy(ref, ref, ss, rs, sib)
 
     def swapped(i):
-        region = a.at[pl.ds(al(oc * ROWS, ROWS), ROWS), pl.ds(al(stripe(i) * STRIPE, STRIPE), STRIPE)]
+        region = a.at[pl.ds(al(oc * ROWS, ROWS), ROWS), pl.ds(al(i * STRIPE, STRIPE), STRIPE)]
         rcopy(region, region, xs.at[0], xr.at[i], sib).wait_recv()
 
+    def item_inverse(lo, hi, sem):
+        all_of(dcr.at[:, pl.ds(lo, hi - lo)], dgs, dgr.at[sem]).wait_recv()
+        for p in range(lo, hi):
+            v = dcs[1, p]
+            for k in range(7):
+                v = v + dcr[k, p]
+            v = lax.rsqrt(jnp.maximum(v, 1.0))
+            for g in range(8):
+                invi[0:1, p * STRIPE + g * 256:p * STRIPE + (g + 1) * 256] = v[g:g + 1, :]
+
+    item_inverse(0, CHIPS - 1, 0)
     all_of(dur, dvs, dvr).wait_recv()
     for blk, v in ((c, dus[...] + dur[0]), (oc, dur[1] + dur[2])):
         v = lax.rsqrt(jnp.maximum(v, 1.0))
         for b in range(ROWS // 128):
-            w = jnp.broadcast_to(v[0:1, b * 128:(b + 1) * 128], (128, 128))
+            w = jnp.broadcast_to(v[b:b + 1, :], (128, 128))
             upart[pl.ds(al(blk * ROWS + b * 128, 128), 128), :] = w.T
-    all_of(dcr, dgs, dgr).wait_recv()
-    for p in range(CHIPS):
-        v = dcs[1, p]
-        for k in range(7):
-            v = v + dcr[k, p]
-        v = lax.rsqrt(jnp.maximum(v, 1.0))
-        for g in range(8):
-            invi[0:1, p * STRIPE + g * 256:p * STRIPE + (g + 1) * 256] = v[g:g + 1, :]
     for i in range(3):
         swapped(i)
 
@@ -258,6 +260,12 @@
         fy = (1 - h) * f2 + h * f1
         return (y + fy - 2 * y * fy) * 2 + (x + fx - 2 * x * fx)
 
+    def in_order(o):
+        h = lax.rem(o, 2)
+        u = lax.div(o, 2)
+        swap = (1 - h) * y * ox + h * oy * x
+        return h + 2 * (u + swap - 2 * u * swap)
+
     def s1(st, t, k, cols=pl.ds(0, CH)):
         h = lax.rem(t, 2)
         to = dev(x + (1 - h) * (1 - 2 * x), y + h * (1 - 2 * y), c, z)
@@ -340,25 +348,28 @@
                 part[t, k] = res[:, k * CH:(k + 1) * CH]
             return 0
 
-        def send_tile(t, _):
+        def send_tile(o, _):
+            t = in_order(o)
             item_tile(t, 0)
             for k in range(NCH):
                 s1(st, t, k).start()
             return 0
 
         def first_chunk(n, _):
-            t = lax.rem(n, 2)
+            h = lax.rem(n, 2)
+            t = in_order(h)
             k = lax.div(n, 2)
-            base = al(tile_q(t) * STRIPE + t * HALF + k * CH, CH)
+            base = al(tile_q(t) * STRIPE + h * HALF + k * CH, CH)
             normalise(base, CH)
             part[t, k] = dot(eut[j], a[:, pl.ds(base, CH)], 1, 0)
             s1(st, t, k).start()
             return 0
 
         def first_half(n, _):
-            t = lax.rem(n, 2)
+            h = lax.rem(n, 2)
+            t = in_order(h)
             cols = pl.ds(al(lax.div(n, 2) * 128, 128), 128)
-            base = al(tile_q(t) * STRIPE + t * HALF + lax.div(n, 2) * 128, 128)
+            base = al(tile_q(t) * STRIPE + h * HALF + lax.div(n, 2) * 128, 128)
             normalise(base, 128)
             part[t, 0, :, cols] = dot(eut[j], a[:, pl.ds(base, 128)], 1, 0)
             s1(st, t, 0, cols).start()
@@ -459,10 +470,10 @@
         if j == 0:
             lax.fori_loop(0, 4, first_half, 0)
             lax.fori_loop(2, 2 * NCH, first_chunk, 0)
+            item_inverse(CHIPS - 1, CHIPS, 1)
+            swapped(CHIPS - 1)
             lax.fori_loop(2, 4, send_tile, 0)
-            lax.fori_loop(4, 6, item_tile, 0)
-            swapped(3)
-            lax.fori_loop(6, 8, item_tile, 0)
+            lax.fori_loop(4, 8, item_tile, 0)
             lax.fori_loop(0, 2, stage1, 0)
             users()
             users_out()
@@ -513,7 +524,7 @@
         all_of(part.at[pl.ds(0, 4)], s1s, s1r.at[0]).wait_send()
         all_of(part.at[pl.ds(4, 2)], s2s, s2r.at[0]).wait_send()
         if j == 0:
-            all_of(dcr, dgs, dgr).wait_send()
+            all_of(dcr, dgs, dgr.at[0]).wait_send()
             all_of(dur, dvs, dvr).wait_send()
             def drain_swap(m, _):
                 xcopy(m).wait_send()
@@ -589,8 +600,8 @@
         pltpu.VMEM((2, 8, STRIPE), F32),
         pltpu.VMEM((2, CHIPS, 8, STRIPE // 8), F32),
         pltpu.VMEM((7, CHIPS, 8, STRIPE // 8), F32),
-        pltpu.VMEM((8, ROWS), F32),
-        pltpu.VMEM((3, 8, ROWS), F32),
+        pltpu.VMEM((8, ROWS // 8), F32),
+        pltpu.VMEM((3, 8, ROWS // 8), F32),
         pltpu.VMEM((UROWS, EMB), F32),
         pltpu.VMEM((QUERIES, EMB), BF),
         pltpu.VMEM((qh, EMB), BF),
@@ -604,7 +615,7 @@
         dma((2,)), dma,
         dma, dma, dma, dma,
         dma, dma((LAYERS,)),
-        dma, dma((3,)), dma, dma, dma, dma,
+        dma, dma((3,)), dma, dma((2,)), dma, dma,
         dma, dma((5,)),
         dma((3,)), dma((2,)), dma,
     ]

time: 175 us -> 175 us (level)
  no operation moved by 1% of the time
where the time goes in v5:
time: 175 us; the launch traced here: 174 us
  Pallas kernels  174 us (99%)
    pallas_call x1, Pallas kernels, propagate(): pl.pallas_call(kernel, out_shape=(jax.ShapeDtypeStruct((UROWS, EMB), BF),...  169 us
    pallas_call x1, Pallas kernels, scores_of(): pl.pallas_call(score_kernel, out_shape=(jax.ShapeDtypeStruct(fu.shape, BF...  4.83 us

profile of v5, /device:TPU:0, one launch (start us, length us, event | category | flops | bytes accessed | tf_op | source)
XLA Modules:
  0.0 174.5 jit_solution(11013593846576265823)
XLA Ops:
  0.6 168.9 %propagate.1 = (bf16[512,128]{1,0:T(8,128)(2,1)}, bf16[2048,128]{1,0:T(8,128)(2,1)}, bf16[1024,128]{1,0:T(8,128)(2,1)}) custom-call(s32[1024,16384]{1,0:T(8,128)} %mask_ref.1, bf16[512,128]{1,0:T(8,128)(2,1)} %ue_hbm.1, bf16[2048,128]{1,0:T(8,128)(2,1)} %ie_hbm.1, s32[1,1024]{1,0:T(1,128)} %bitcast.1), custom_call_target="tpu_custom_call" | custom-call | tf_op jit(solution)/shard_map/propagate/pallas_call | solution.py:622
  169.5 4.8 %scores.1 = (bf16[512,128]{1,0:T(8,128)(2,1)}, bf16[2048,128]{1,0:T(8,128)(2,1)}, f32[1024,2048]{1,0:T(8,128)}) custom-call(bf16[512,128]{1,0:T(8,128)(2,1)} %get-tuple-element.6.fu_ref, bf16[2048,128]{1,0:T(8,128)(2,1)} %get-tuple-element.7.fi_ref, bf16[1024,128]{1,0:T(8,128)(2,1)} %get-tuple-element.8.pk_ref), custom_call_target="tpu_custom_call" | custom-call | tf_op jit(solution)/shard_map/scores/pallas_call | solution.py:565

commit v6 on v5

--- a/solution.py
+++ b/solution.py
@@ -35,11 +35,11 @@
     return lax.dot_general(a, b, (((ca,), (cb,)), ((), ())), preferred_element_type=F32)
 
 
-def kernel(mask_ref, ue_hbm, ie_hbm, q_hbm, fu_hbm, fi_hbm, pk_hbm, ue_ref, ie_ref, q_ref, fu_ref, fi_ref, pkf,
+def kernel(mask_ref, ue_hbm, ie_hbm, q_hbm, fu_ref, fi_ref, pk_ref, ue_ref, ie_ref, q_ref, pkf,
            a, part, r1, r2, panel, eut, upart, ursib, urz, invi, mbuf, stage,
            cs, dcs, dcr, dus, dur, usum, pkc, pks, pkz, pkx, pka,
            lsem, xs, xr, s1s, s1r, s2s, s2r, ags, agr, fws, fwr,
-           usibs, usibr, uzs, uzr, uas, uar, eis, eir, dgs, dgr, dvs, dvr, pqs, pqr, ins, outs, fis):
+           usibs, usibr, uzs, uzr, uas, uar, eis, eir, dgs, dgr, dvs, dvr, pqs, pqr, ins):
     row = lax.axis_index('row')
     z = lax.axis_index('col')
     c = lax.rem(row, 2)
@@ -324,16 +324,6 @@
             return 0
         lax.fori_loop(0, 2 * ROWS // 128, norm, 0)
 
-    def fu_out():
-        return pltpu.make_async_copy(fu_ref, fu_hbm, outs.at[0])
-
-    def pk_out():
-        return pltpu.make_async_copy(pkf, pk_hbm, outs.at[1])
-
-    def fi_out(h, k):
-        loc = pl.ds(al(h * HALF + k * CH, CH), CH)
-        return pltpu.make_async_copy(fi_ref.at[loc], fi_hbm.at[loc], fis)
-
     for j in range(LAYERS):
         st = j % 2
         last = j == LAYERS - 1
@@ -393,7 +383,6 @@
                     tot = ie_ref[loc, :].astype(F32) + panel[1, rsl, :].astype(F32)
                     tot = tot + panel[0, rsl, :].astype(F32) + e.astype(F32)
                     fi_ref[loc, :] = (tot * (1.0 / (LAYERS + 1))).astype(BF)
-                    fi_out(h, k).start()
                 else:
                     panel[1 - st, rsl, :] = e
                     ag(st, 0, h, k).start()
@@ -461,7 +450,6 @@
                 return
             fu = (usum[...] * (1.0 / (LAYERS + 1))).astype(BF)
             fu_ref[...] = fu
-            fu_out().start()
             ids = lax.broadcasted_iota(jnp.int32, (UROWS, QUERIES), 0) + (row * 2 + z) * UROWS
             hot = jnp.where(ids == q_ref[...], 1.0, 0.0).astype(BF)
             pkc[...] = dot(hot, fu, 0, 0).astype(BF)
@@ -536,11 +524,8 @@
             all_of(panel.at[st, pl.ds(0, STRIPE)], fws.at[1 - st], fwr).wait_send()
 
     all_of(pkf.at[pl.ds(0, 3 * qq)], pqs, pqr.at[4]).wait_recv()
-    pk_out().start()
-    all_of(fi_ref, pqs, pqr.at[4]).wait_send()
-    pltpu.make_async_copy(fi_ref, fi_hbm, fis).wait()
-    fu_out().wait()
-    pk_out().wait()
+    pk_ref[...] = pkf[...]
+    all_of(ie_ref, pqs, pqr.at[4]).wait_send()
 
 
 def score_kernel(fu_ref, fi_ref, pk_ref, fu_out, fi_out, s_out, buf, sem, out_sem):
@@ -570,20 +555,20 @@
         out_specs=(hbm, hbm, hbm),
         scratch_shapes=[pltpu.VMEM((QUERIES // SROWS, SROWS, STRIPE), F32),
                         pltpu.SemaphoreType.DMA((QUERIES // SROWS,)), pltpu.SemaphoreType.DMA((2,))],
+        compiler_params=pltpu.CompilerParams(vmem_limit_bytes=16 * 1024 * 1024),
         name='scores',
     )(fu, fi, picked)
 
 
 def propagate(mask_blk, user_shard, item_shard, queries):
     hbm = pl.BlockSpec(memory_space=pl.ANY)
+    vm = pl.BlockSpec(memory_space=pltpu.VMEM)
     dma = pltpu.SemaphoreType.DMA
     qh, qq = QUERIES // 2, QUERIES // 4
     scratch = [
         pltpu.VMEM((UROWS, EMB), BF),
         pltpu.VMEM((STRIPE, EMB), BF),
         pltpu.VMEM((1, QUERIES), jnp.int32),
-        pltpu.VMEM((UROWS, EMB), BF),
-        pltpu.VMEM((STRIPE, EMB), BF),
         pltpu.VMEM((QUERIES, EMB), BF),
         pltpu.VMEM((2 * ROWS, COLS), BF),
         pltpu.VMEM((8, NCH, EMB, CH), F32),
@@ -617,18 +602,16 @@
         dma, dma((LAYERS,)),
         dma, dma((3,)), dma, dma((2,)), dma, dma,
         dma, dma((5,)),
-        dma((3,)), dma((2,)), dma,
+        dma((3,)),
     ]
     return pl.pallas_call(
         kernel,
-        out_shape=(jax.ShapeDtypeStruct((UROWS, EMB), BF),
-                   jax.ShapeDtypeStruct((STRIPE, EMB), BF),
-                   jax.ShapeDtypeStruct((QUERIES, EMB), BF)),
+        out_shape=(pltpu.VMEM((UROWS, EMB), BF), pltpu.VMEM((STRIPE, EMB), BF), pltpu.VMEM((QUERIES, EMB), BF)),
         in_specs=[hbm] * 4,
-        out_specs=(hbm, hbm, hbm),
+        out_specs=(vm, vm, vm),
         scratch_shapes=scratch,
         compiler_params=pltpu.CompilerParams(collective_id=0, has_side_effects=True,
-                                             vmem_limit_bytes=67043328),
+                                             vmem_limit_bytes=64487424),
         name='propagate',
     )(mask_blk, user_shard, item_shard, queries)
 

time: 175 us -> 173 us (0.989)
  Pallas kernels: 174 us -> 172 us
where the time goes in v6:
time: 173 us
  Pallas kernels  172 us (99%)
    pallas_call x1, Pallas kernels, propagate(): pl.pallas_call(kernel, out_shape=(pltpu.VMEM((UROWS, EMB), BF), pltpu.VME...  168 us
    pallas_call x1, Pallas kernels, scores_of(): pl.pallas_call(score_kernel, out_shape=(jax.ShapeDtypeStruct(fu.shape, BF...  3.9 us

profile of v6, /device:TPU:0, one launch (start us, length us, event | category | flops | bytes accessed | tf_op | source)
XLA Modules:
  0.0 172.8 jit_solution(1816178339913676354)
XLA Ops:
  0.6 168.1 %propagate.1 = (bf16[512,128]{1,0:T(8,128)(2,1)S(1)}, bf16[2048,128]{1,0:T(8,128)(2,1)S(1)}, bf16[1024,128]{1,0:T(8,128)(2,1)S(1)}) custom-call(s32[1024,16384]{1,0:T(8,128)} %mask_ref.1, bf16[512,128]{1,0:T(8,128)(2,1)} %ue_hbm.1, bf16[2048,128]{1,0:T(8,128)(2,1)} %ie_hbm.1, s32[1,1024]{1,0:T(1,128)} %bitcast.1), custom_call_target="tpu_custom_call" | custom-call | tf_op jit(solution)/shard_map/propagate/pallas_call | solution.py:607
  168.7 3.9 %scores.1 = (bf16[512,128]{1,0:T(8,128)(2,1)}, bf16[2048,128]{1,0:T(8,128)(2,1)}, f32[1024,2048]{1,0:T(8,128)}) custom-call(bf16[512,128]{1,0:T(8,128)(2,1)S(1)} %get-tuple-element.6.fu_ref, bf16[2048,128]{1,0:T(8,128)(2,1)S(1)} %get-tuple-element.7.fi_ref, bf16[1024,128]{1,0:T(8,128)(2,1)S(1)} %get-tuple-element.8.pk_ref), custom_call_target="tpu_custom_call" | custom-call | tf_op jit(solution)/shard_map/scores/pallas_call | solution.py:550

commit v7 on v6

--- a/solution.py
+++ b/solution.py
@@ -38,8 +38,8 @@
 def kernel(mask_ref, ue_hbm, ie_hbm, q_hbm, fu_ref, fi_ref, pk_ref, ue_ref, ie_ref, q_ref, pkf,
            a, part, r1, r2, panel, eut, upart, ursib, urz, invi, mbuf, stage,
            cs, dcs, dcr, dus, dur, usum, pkc, pks, pkz, pkx, pka,
-           lsem, xs, xr, s1s, s1r, s2s, s2r, ags, agr, fws, fwr,
-           usibs, usibr, uzs, uzr, uas, uar, eis, eir, dgs, dgr, dvs, dvr, pqs, pqr, ins):
+           lsem, xs, xr, s1s, s1r, s2s, ags, agr, fws, fwr,
+           usibs, usibr, uzs, uzr, uas, uar, eis, eir, dgs, dgr, dvs, dvr, pqs, ins):
     row = lax.axis_index('row')
     z = lax.axis_index('col')
     c = lax.rem(row, 2)
@@ -129,7 +129,7 @@
                      (xn, yn, dg, sib, xnc, ync, dgc)[i])
 
     def dusend(i):
-        return rcopy(dus, dur.at[i], dvs, dvr, (zn, sib, zsib)[i])
+        return rcopy(dus, dur.at[i], dvs, dvr.at[min(i, 1)], (zn, sib, zsib)[i])
 
     def stripe_degrees(p, par):
         v = jnp.sum(cs[par], axis=0, keepdims=True)
@@ -243,12 +243,16 @@
                 invi[0:1, p * STRIPE + g * 256:p * STRIPE + (g + 1) * 256] = v[g:g + 1, :]
 
     item_inverse(0, CHIPS - 1, 0)
-    all_of(dur, dvs, dvr).wait_recv()
-    for blk, v in ((c, dus[...] + dur[0]), (oc, dur[1] + dur[2])):
+    def user_inverse(blk, v):
         v = lax.rsqrt(jnp.maximum(v, 1.0))
         for b in range(ROWS // 128):
             w = jnp.broadcast_to(v[b:b + 1, :], (128, 128))
             upart[pl.ds(al(blk * ROWS + b * 128, 128), 128), :] = w.T
+
+    dusend(0).wait_recv()
+    user_inverse(c, dus[...] + dur[0])
+    all_of(dur.at[pl.ds(1, 2)], dvs, dvr.at[1]).wait_recv()
+    user_inverse(oc, dur[1] + dur[2])
     for i in range(3):
         swapped(i)
 
@@ -272,7 +276,7 @@
         return rcopy(part.at[t, k, :, cols], r1.at[t, k, :, cols], s1s, s1r.at[k], to)
 
     def s2(st, h, k):
-        return rcopy(part.at[4 + h, k], r2.at[h, k], s2s, s2r.at[k], (yn, xn)[h])
+        return rcopy(part.at[4 + h, k], r2.at[h, k], s2s, xr.at[k], (yn, xn)[h])
 
     def chunk_rows(q, h, k):
         return pl.ds(al(q * STRIPE + h * HALF + k * CH, CH), CH)
@@ -298,18 +302,18 @@
     quarter = pl.ds(al(c * qh + z * qq, qq), qq)
 
     def pq_sib():
-        return rcopy(pkc.at[pl.ds(al(oc * qh, qh), qh)], pks, pqs, pqr.at[0], sib)
+        return rcopy(pkc.at[pl.ds(al(oc * qh, qh), qh)], pks, pqs, xs.at[0], sib)
 
     def pq_z():
-        return rcopy(pkc.at[pl.ds(al(c * qh + oz * qq, qq), qq)], pkz, pqs, pqr.at[1], zn)
+        return rcopy(pkc.at[pl.ds(al(c * qh + oz * qq, qq), qq)], pkz, pqs, xs.at[1], zn)
 
     def pq_x(i):
         h, to = ((0, xn), (1, yn), (0, yn), (1, xn))[i]
         src = (pkc if i < 2 else pka).at[pl.ds(al(c * qh + z * qq + h * (qq // 2), qq // 2), qq // 2)]
-        return rcopy(src, pkx.at[i], pqs, pqr.at[2 + i // 2], to)
+        return rcopy(src, pkx.at[i], pqs, xs.at[2 + i // 2], to)
 
     def pq_a(i):
-        return rcopy(pkf.at[quarter], pkf.at[quarter], pqs, pqr.at[4], (zn, sib, zsib)[i])
+        return rcopy(pkf.at[quarter], pkf.at[quarter], pqs, xs.at[4], (zn, sib, zsib)[i])
 
     def badd(u, v):
         return (u.astype(F32) + v.astype(F32)).astype(BF)
@@ -374,7 +378,7 @@
             return 0
 
         def stage2(k, _):
-            all_of(r2.at[:, k], s2s, s2r.at[k]).wait_recv()
+            all_of(r2.at[:, k], s2s, xr.at[k]).wait_recv()
             for h in range(2):
                 e = (part[6 + h, k] + r2[h, k]).T.astype(BF)
                 rsl = chunk_rows(me, h, k)
@@ -487,7 +491,7 @@
                 for i in range(2):
                     pq_x(i).start()
                 stage1(1, 0)
-                all_of(pkx.at[pl.ds(0, 2)], pqs, pqr.at[2]).wait_recv()
+                all_of(pkx.at[pl.ds(0, 2)], pqs, xs.at[2]).wait_recv()
                 for i in range(2):
                     rsl = pl.ds(al(c * qh + z * qq + i * (qq // 2), qq // 2), qq // 2)
                     pka[rsl, :] = badd(pkc[rsl, :], pkx[i])
@@ -496,7 +500,7 @@
             lax.fori_loop(2, NCH, stage1, 0)
             lax.fori_loop(0, 2, stage2, 0)
             if last:
-                all_of(pkx.at[pl.ds(2, 2)], pqs, pqr.at[3]).wait_recv()
+                all_of(pkx.at[pl.ds(2, 2)], pqs, xs.at[3]).wait_recv()
                 for i in range(2, 4):
                     rsl = pl.ds(al(c * qh + z * qq + (i - 2) * (qq // 2), qq // 2), qq // 2)
                     pkf[rsl, :] = badd(pka[rsl, :], pkx[i])
@@ -510,10 +514,10 @@
         uz(j).wait_send()
         all_of(eut.at[j, :, pl.ds(0, 3 * UROWS)], uas, uar.at[j]).wait_send()
         all_of(part.at[pl.ds(0, 4)], s1s, s1r.at[0]).wait_send()
-        all_of(part.at[pl.ds(4, 2)], s2s, s2r.at[0]).wait_send()
+        all_of(part.at[pl.ds(4, 2)], s2s, xr.at[0]).wait_send()
         if j == 0:
             all_of(dcr, dgs, dgr.at[0]).wait_send()
-            all_of(dur, dvs, dvr).wait_send()
+            all_of(dur, dvs, dvr.at[0]).wait_send()
             def drain_swap(m, _):
                 xcopy(m).wait_send()
                 return 0
@@ -523,25 +527,24 @@
             all_of(panel.at[st, pl.ds(0, 2 * STRIPE)], ags.at[1 - st], agr.at[NCH]).wait_send()
             all_of(panel.at[st, pl.ds(0, STRIPE)], fws.at[1 - st], fwr).wait_send()
 
-    all_of(pkf.at[pl.ds(0, 3 * qq)], pqs, pqr.at[4]).wait_recv()
+    all_of(pkf.at[pl.ds(0, 3 * qq)], pqs, xs.at[4]).wait_recv()
     pk_ref[...] = pkf[...]
-    all_of(ie_ref, pqs, pqr.at[4]).wait_send()
+    all_of(ie_ref, pqs, xs.at[4]).wait_send()
 
 
 def score_kernel(fu_ref, fi_ref, pk_ref, fu_out, fi_out, s_out, buf, sem, out_sem):
-    copies = [pltpu.make_async_copy(fu_ref, fu_out, out_sem.at[0]),
-              pltpu.make_async_copy(fi_ref, fi_out, out_sem.at[1])]
+    small = [pltpu.make_async_copy(fu_ref, fu_out, out_sem.at[0]),
+             pltpu.make_async_copy(fi_ref, fi_out, out_sem.at[1])]
     for i in range(QUERIES // SROWS):
         rsl = pl.ds(i * SROWS, SROWS)
-        buf[i] = dot(pk_ref[rsl, :], fi_ref[...], 1, 1)
-        copies.append(pltpu.make_async_copy(buf.at[i], s_out.at[rsl, :], sem.at[i]))
+        buf[rsl, :] = dot(pk_ref[rsl, :], fi_ref[...], 1, 1)
+        pltpu.make_async_copy(buf.at[rsl], s_out.at[rsl, :], sem).start()
         if i == 0:
-            for cp in copies:
+            for cp in small:
                 cp.start()
-        else:
-            copies[-1].start()
-    for cp in copies:
+    for cp in small:
         cp.wait()
+    pltpu.make_async_copy(buf, s_out, sem).wait()
 
 
 def scores_of(fu, fi, picked):
@@ -553,8 +556,8 @@
                    jax.ShapeDtypeStruct((QUERIES, STRIPE), F32)),
         in_specs=[vm, vm, vm],
         out_specs=(hbm, hbm, hbm),
-        scratch_shapes=[pltpu.VMEM((QUERIES // SROWS, SROWS, STRIPE), F32),
-                        pltpu.SemaphoreType.DMA((QUERIES // SROWS,)), pltpu.SemaphoreType.DMA((2,))],
+        scratch_shapes=[pltpu.VMEM((QUERIES, STRIPE), F32),
+                        pltpu.SemaphoreType.DMA, pltpu.SemaphoreType.DMA((2,))],
         compiler_params=pltpu.CompilerParams(vmem_limit_bytes=16 * 1024 * 1024),
         name='scores',
     )(fu, fi, picked)
@@ -594,14 +597,13 @@
         pltpu.VMEM((4, qq // 2, EMB), BF),
         pltpu.VMEM((QUERIES, EMB), BF),
         dma((NLOAD,)), dma((NSTAGE,)), dma((CHIPS,)),
-        dma, dma((NCH,)),
-        dma, dma((NCH,)),
+        dma, dma((NCH,)), dma,
         dma((2,)), dma((NCH + 1,)),
         dma((2,)), dma,
         dma, dma, dma, dma,
         dma, dma((LAYERS,)),
-        dma, dma((3,)), dma, dma((2,)), dma, dma,
-        dma, dma((5,)),
+        dma, dma((3,)), dma, dma((2,)), dma, dma((2,)),
+        dma,
         dma((3,)),
     ]
     return pl.pallas_call(

time: 173 us -> 173 us (level)
  no operation moved by 1% of the time
where the time goes in v7:
time: 173 us
  Pallas kernels  172 us (99%)
    pallas_call x1, Pallas kernels, propagate(): pl.pallas_call(kernel, out_shape=(pltpu.VMEM((UROWS, EMB), BF), pltpu.VME...  168 us
    pallas_call x1, Pallas kernels, scores_of(): pl.pallas_call(score_kernel, out_shape=(jax.ShapeDtypeStruct(fu.shape, BF...  3.84 us

profile of v7, /device:TPU:0, one launch (start us, length us, event | category | flops | bytes accessed | tf_op | source)
XLA Modules:
  0.0 172.5 jit_solution(15094199219957709113)
XLA Ops:
  0.6 167.9 %propagate.1 = (bf16[512,128]{1,0:T(8,128)(2,1)S(1)}, bf16[2048,128]{1,0:T(8,128)(2,1)S(1)}, bf16[1024,128]{1,0:T(8,128)(2,1)S(1)}) custom-call(s32[1024,16384]{1,0:T(8,128)} %mask_ref.1, bf16[512,128]{1,0:T(8,128)(2,1)} %ue_hbm.1, bf16[2048,128]{1,0:T(8,128)(2,1)} %ie_hbm.1, s32[1,1024]{1,0:T(1,128)} %bitcast.1), custom_call_target="tpu_custom_call" | custom-call | tf_op jit(solution)/shard_map/propagate/pallas_call | solution.py:609
  168.5 3.8 %scores.1 = (bf16[512,128]{1,0:T(8,128)(2,1)}, bf16[2048,128]{1,0:T(8,128)(2,1)}, f32[1024,2048]{1,0:T(8,128)}) custom-call(bf16[512,128]{1,0:T(8,128)(2,1)S(1)} %get-tuple-element.6.fu_ref, bf16[2048,128]{1,0:T(8,128)(2,1)S(1)} %get-tuple-element.7.fi_ref, bf16[1024,128]{1,0:T(8,128)(2,1)S(1)} %get-tuple-element.8.pk_ref), custom_call_target="tpu_custom_call" | custom-call | tf_op jit(solution)/shard_map/scores/pallas_call | solution.py:553

commit v8 on v7

--- a/solution.py
+++ b/solution.py
@@ -20,7 +20,7 @@
 NCH = 4
 CH = HALF // NCH
 LROWS = 128
-NLOAD = 6
+NLOAD = 7
 NSTAGE = 11
 N_HELD = 8
 QUERIES = 1024
@@ -613,7 +613,7 @@
         out_specs=(vm, vm, vm),
         scratch_shapes=scratch,
         compiler_params=pltpu.CompilerParams(collective_id=0, has_side_effects=True,
-                                             vmem_limit_bytes=64487424),
+                                             vmem_limit_bytes=65929216),
         name='propagate',
     )(mask_blk, user_shard, item_shard, queries)
 

time: 173 us -> 173 us (level)
  no operation moved by 1% of the time
where the time goes in v8:
time: 173 us; the launch traced here: 172 us
  Pallas kernels  172 us (99%)
    pallas_call x1, Pallas kernels, propagate(): pl.pallas_call(kernel, out_shape=(pltpu.VMEM((UROWS, EMB), BF), pltpu.VME...  168 us
    pallas_call x1, Pallas kernels, scores_of(): pl.pallas_call(score_kernel, out_shape=(jax.ShapeDtypeStruct(fu.shape, BF...  3.84 us

profile of v8, /device:TPU:0, one launch (start us, length us, event | category | flops | bytes accessed | tf_op | source)
XLA Modules:
  0.0 172.5 jit_solution(11878598652996337892)
XLA Ops:
  0.6 167.9 %propagate.1 = (bf16[512,128]{1,0:T(8,128)(2,1)S(1)}, bf16[2048,128]{1,0:T(8,128)(2,1)S(1)}, bf16[1024,128]{1,0:T(8,128)(2,1)S(1)}) custom-call(s32[1024,16384]{1,0:T(8,128)} %mask_ref.1, bf16[512,128]{1,0:T(8,128)(2,1)} %ue_hbm.1, bf16[2048,128]{1,0:T(8,128)(2,1)} %ie_hbm.1, s32[1,1024]{1,0:T(1,128)} %bitcast.1), custom_call_target="tpu_custom_call" | custom-call | tf_op jit(solution)/shard_map/propagate/pallas_call | solution.py:609
  168.5 3.8 %scores.1 = (bf16[512,128]{1,0:T(8,128)(2,1)}, bf16[2048,128]{1,0:T(8,128)(2,1)}, f32[1024,2048]{1,0:T(8,128)}) custom-call(bf16[512,128]{1,0:T(8,128)(2,1)S(1)} %get-tuple-element.6.fu_ref, bf16[2048,128]{1,0:T(8,128)(2,1)S(1)} %get-tuple-element.7.fi_ref, bf16[1024,128]{1,0:T(8,128)(2,1)S(1)} %get-tuple-element.8.pk_ref), custom_call_target="tpu_custom_call" | custom-call | tf_op jit(solution)/shard_map/scores/pallas_call | solution.py:553
